TPU v7x, 32 devices: a whole 2x2x4 slice. The times are simulated.
32 devices in a mesh: seq: 8 (over y, x, core), kvh: 4 (over z).
Axes of the slice: x: 2, y: 2, z: 4, core: 2. Of those that a mesh axis runs over, the one named last changes fastest.
Arguments:
- queries: bfloat16 [64, 32, 128], P(('seq', 'kvh')), may hold values from -9 to 9
- attn_out: bfloat16 [64, 32, 128], P(('seq', 'kvh')), may hold values from -0.59765625 to 0.59765625
- grad_out: bfloat16 [64, 32, 128], P(('seq', 'kvh')), may hold values from -384 to 384
- log_norms: float32 [64, 32], P(('seq', 'kvh')), may hold values from 0 to 14, as said below
- query_starts: int32 [64], replicated, may hold values from 0 to 2048
- keys: bfloat16 [8192, 4, 128], P('seq', 'kvh'), may hold values from -6 to 6
- values: bfloat16 [8192, 4, 128], P('seq', 'kvh'), may hold values from -6 to 6
Outputs:
- grad_query: bfloat16 [64, 32, 128], P(('seq', 'kvh'))
- grad_keys: bfloat16 [8192, 4, 128], P('seq', 'kvh')
- grad_values: bfloat16 [8192, 4, 128], P('seq', 'kvh')
Inputs may be any that keep to these rules, and one draw needn't show every extreme that they name: `log_norms`: each entry lies within one of the log of its token's number of visible positions plus 1.125.
All inputs are finite; a program needn't handle non-finite values.
Results may differ from a plain program's by a relative error of at most 0.0052.
Values may be sent and summed in bfloat16 or wider, within the bound.
No kernel may reach another device: no remote copies, remote signals or barrier semaphores. Data moves between devices by JAX's collectives and lax.ppermute only.
A program may use at most 64 MiB of HBM per device.

v0:
```python
import jax
import jax.numpy as jnp
from jax import lax
from jax.sharding import PartitionSpec as P


def shifted(value, axis, by):
    peers = lax.axis_size(axis)
    return lax.ppermute(value, axis, [(i, (i + by) % peers) for i in range(peers)])


def local(queries, attn_out, grad_out, log_norms, query_starts, keys, values):
    scaling = queries.shape[-1] ** (-0.5)
    seq_count = lax.axis_size("seq")
    seq_index = lax.axis_index("seq")
    deltas = jnp.sum(grad_out.astype(jnp.float32) * attn_out.astype(jnp.float32), axis=-1)
    query_block, grad_block = (
        lax.all_to_all(queries, "kvh", split_axis=1, concat_axis=0, tiled=True),
        lax.all_to_all(grad_out, "kvh", split_axis=1, concat_axis=0, tiled=True),
    )
    norm_block, delta_block = (
        lax.all_to_all(log_norms, "kvh", split_axis=1, concat_axis=0, tiled=True),
        lax.all_to_all(deltas, "kvh", split_axis=1, concat_axis=0, tiled=True),
    )
    block_rows = query_block.shape[0]
    total_rows = block_rows * seq_count
    key_count = keys.shape[0]
    key_rows = keys[:, 0, :]
    value_rows = values[:, 0, :]
    key_pos = seq_index * key_count + jnp.arange(key_count, dtype=jnp.int32)
    offset = key_count * seq_count - total_rows

    def block_terms(queries_in, grads_in, norms_in, deltas_in, first_row):
        row_count = queries_in.shape[0]
        query_pos = offset + first_row + jnp.arange(row_count, dtype=jnp.int32)
        first_keys = lax.dynamic_slice_in_dim(query_starts, first_row, row_count)
        visible = (key_pos[None, :] >= first_keys[:, None]) & (
            key_pos[None, :] <= query_pos[:, None]
        )
        scores = (
            jnp.einsum("rgd,kd->rgk", queries_in, key_rows, preferred_element_type=jnp.float32)
            * scaling
        )
        weights = jnp.where(visible[:, None, :], jnp.exp(scores - norms_in[..., None]), 0.0)
        weight_grad = jnp.einsum(
            "rgd,kd->rgk", grads_in, value_rows, preferred_element_type=jnp.float32
        )
        score_grad = weights * (weight_grad - deltas_in[..., None])
        weight_half = weights.astype(jnp.bfloat16)
        score_half = score_grad.astype(jnp.bfloat16)
        value_part = jnp.einsum(
            "rgk,rgd->kd", weight_half, grads_in, preferred_element_type=jnp.float32
        )
        key_part = (
            jnp.einsum("rgk,rgd->kd", score_half, queries_in, preferred_element_type=jnp.float32)
            * scaling
        )
        query_part = (
            jnp.einsum("rgk,kd->rgd", score_half, key_rows, preferred_element_type=jnp.float32)
            * scaling
        )
        return (key_part, value_part, query_part)

    key_empty = jnp.zeros(key_rows.shape, jnp.float32)

    def visit_owner(counter, carried):
        query_now, grad_now, norm_now, delta_now, query_grad, key_grad, value_grad = carried
        anchor = (seq_index - counter) % seq_count
        key_part, value_part, query_part = block_terms(
            query_now, grad_now, norm_now, delta_now, anchor * block_rows
        )
        query_now, grad_now = shifted((query_now, grad_now), "seq", 1)
        norm_now, delta_now, query_grad = shifted(
            (norm_now, delta_now, query_grad + query_part), "seq", 1
        )
        return (
            query_now,
            grad_now,
            norm_now,
            delta_now,
            query_grad,
            key_grad + key_part,
            value_grad + value_part,
        )

    query_empty = jnp.zeros(query_block.shape, jnp.float32)
    carried = (query_block, grad_block, norm_block, delta_block, query_empty, key_empty, key_empty)
    carried = lax.fori_loop(0, seq_count - 1, visit_owner, carried)
    query_now, grad_now, norm_now, delta_now, query_grad, key_grad, value_grad = carried
    anchor = (seq_index + 1) % seq_count
    key_part, value_part, query_part = block_terms(
        query_now, grad_now, norm_now, delta_now, anchor * block_rows
    )
    key_grad = key_grad + key_part
    value_grad = value_grad + value_part
    query_grad = shifted((query_grad + query_part).astype(jnp.bfloat16), "seq", 1).astype(
        jnp.float32
    )
    grad_query = lax.all_to_all(
        query_grad.astype(jnp.bfloat16), "kvh", split_axis=0, concat_axis=1, tiled=True
    )
    return (
        grad_query,
        key_grad.astype(jnp.bfloat16)[:, None, :],
        value_grad.astype(jnp.bfloat16)[:, None, :],
    )


def solution(mesh):
    return jax.shard_map(
        local,
        mesh=mesh,
        in_specs=(
            P(("seq", "kvh"), None, None),
            P(("seq", "kvh"), None, None),
            P(("seq", "kvh"), None, None),
            P(("seq", "kvh"), None),
            P(),
            P("seq", "kvh", None),
            P("seq", "kvh", None),
        ),
        out_specs=(P(("seq", "kvh"), None, None), P("seq", "kvh", None), P("seq", "kvh", None)),
        check_vma=False,
    )
```

profile of v0, /device:TPU:0, one launch (start us, length us, event | category | flops | bytes accessed | tf_op | source)
XLA Modules:
  0.0 116.3 jit_solution(9681202412714350968)
XLA Ops:
  0.7 0.8 all_to_all.75
  1.5 0.6 copy.31
  2.1 6.3 %all-to-all-start.2 = ((f32[2,4,8]{2,0,1:T(2,128)}), f32[2,4,8]{2,0,1:T(2,128)S(1)}, u32[]{:S(2)}, u32[]{:S(2)}) async-start(f32[2,4,8]{2,0,1:T(2,128)} %copy.31), calls=%async_computation.2 | async-start | bytes 8192 | tf_op jit(solution)/shard_map/all_to_all | solution.py:22
  8.4 0.6 copy.27
  9.0 0.7 dynamic_slice.13
  9.8 4.2 %all-to-all-done.2 = f32[2,4,8]{2,0,1:T(2,128)S(1)} async-done(((f32[2,4,8]{2,0,1:T(2,128)}), f32[2,4,8]{2,0,1:T(2,128)S(1)}, u32[]{:S(2)}, u32[]{:S(2)}) %all-to-all-start.2) | async-done | bytes 288 | tf_op jit(solution)/shard_map/all_to_all | solution.py:22
  14.0 3.3 %all-to-all-start = ((bf16[2,32,128]{2,0,1:T(2,128)(2,1)}), bf16[2,32,128]{2,0,1:T(2,128)(2,1)S(1)}, u32[]{:S(2)}, u32[]{:S(2)}) async-start(bf16[2,32,128]{2,0,1:T(2,128)(2,1)} %copy.27), calls=%async_computation | async-start | bytes 32768 | tf_op jit(solution)/shard_map/all_to_all | solution.py:18
  17.3 1.3 %copy.29 = bf16[2,32,128]{2,0,1:T(2,128)(2,1)} copy(bf16[2,32,128]{2,1,0:T(8,128)(2,1)} %param.11) | data formatting | bytes 32768 | tf_op args[2]
  18.7 4.2 %all-to-all-done = bf16[2,32,128]{2,0,1:T(2,128)(2,1)S(1)} async-done(((bf16[2,32,128]{2,0,1:T(2,128)(2,1)}), bf16[2,32,128]{2,0,1:T(2,128)(2,1)S(1)}, u32[]{:S(2)}, u32[]{:S(2)}) %all-to-all-start) | async-done | bytes 16416 | tf_op jit(solution)/shard_map/all_to_all | solution.py:18
  22.8 3.3 %all-to-all-start.1 = ((bf16[2,32,128]{2,0,1:T(2,128)(2,1)}), bf16[2,32,128]{2,0,1:T(2,128)(2,1)S(1)}, u32[]{:S(2)}, u32[]{:S(2)}) async-start(bf16[2,32,128]{2,0,1:T(2,128)(2,1)} %copy.29), calls=%async_computation.1 | async-start | bytes 32768 | tf_op jit(solution)/shard_map/all_to_all | solution.py:19
  26.1 0.8 multiply_reduce_fusion
  27.0 0.6 copy.32
  27.6 4.1 %all-to-all-done.1 = bf16[2,32,128]{2,0,1:T(2,128)(2,1)S(1)} async-done(((bf16[2,32,128]{2,0,1:T(2,128)(2,1)}), bf16[2,32,128]{2,0,1:T(2,128)(2,1)S(1)}, u32[]{:S(2)}, u32[]{:S(2)}) %all-to-all-start.1) | async-done | bytes 16416 | tf_op jit(solution)/shard_map/all_to_all | solution.py:19
  31.7 3.2 %all-to-all-start.3 = ((f32[2,4,8]{2,0,1:T(2,128)}), f32[2,4,8]{2,0,1:T(2,128)S(1)}, u32[]{:S(2)}, u32[]{:S(2)}) async-start(f32[2,4,8]{2,0,1:T(2,128)} %copy.32), calls=%async_computation.3 | async-start | bytes 8192 | tf_op jit(solution)/shard_map/all_to_all | solution.py:23
  35.0 5.5 %all-to-all-done.3 = f32[2,4,8]{2,0,1:T(2,128)S(1)} async-done(((f32[2,4,8]{2,0,1:T(2,128)}), f32[2,4,8]{2,0,1:T(2,128)S(1)}, u32[]{:S(2)}, u32[]{:S(2)}) %all-to-all-start.3) | async-done | bytes 288 | tf_op jit(solution)/shard_map/all_to_all | solution.py:23
  40.5 0.6 copy-done.4
  41.1 60.2 %while.28 = (s32[]{:T(128)}, bf16[8,8,128]{2,0,1:T(8,128)(2,1)S(1)}, bf16[8,8,128]{2,0,1:T(8,128)(2,1)S(1)}, f32[8,8]{1,0:T(8,128)S(1)}, f32[8,8]{1,0:T(8,128)S(...) while((s32[]{:T(128)}, ...), condition=%wide.region_2.3_spmd.clone, body=%wide.region_1.2_spmd.clone.sunk | while | flops 85042200 | bytes 5599483 | solution.py:88
  41.1 1.6 %collective-permute-start.1 = (bf16[8,8,128]{2,0,1:T(8,128)(2,1)S(1)}, bf16[8,8,128]{2,0,1:T(8,128)(2,1)S(1)}, u32[]{:S(2)}, u32[]{:S(2)}) collective-permute-start(bf16[8,8,128]{2,0,1:T(8,128)(2,1)S(1)} %copy.78), channel_id=1, source_target_pairs={{0,4},{4,8},{8,12},{12,16},{16,20},{20,24},{24,28},{28,0},{1,5},{5... | collective-permute-start | bytes 49160 | tf_op jit(solution)/shard_map/while/body/eval_jaxpr/ppermute | solution.py:9
  42.8 1.5 %collective-permute-start.3 = (f32[8,8]{1,0:T(8,128)S(1)}, f32[8,8]{1,0:T(8,128)S(1)}, u32[]{:S(2)}, u32[]{:S(2)}) collective-permute-start(f32[8,8]{1,0:T(8,128)S(1)} %copy.80), channel_id=1, source_target_pairs={{0,4},{4,8},{8,12},{12,16},{16,20},{20,24},{24,28},{28,0},{1,5},{5... | collective-permute-start | bytes 776 | tf_op jit(solution)/shard_map/while/body/eval_jaxpr/ppermute | solution.py:9
  44.7 0.7 copy-done.1
  46.0 0.3 fusion.74
  46.3 0.3 fusion.73
  46.7 3.4 %collective-permute-done.4 = f32[8,8,128]{2,1,0:T(8,128)S(1)} collective-permute-done((f32[8,8,128]{2,1,0:T(8,128)S(1)}, f32[8,8,128]{2,1,0:T(8,128)S(1)}, u32[]{:S(2)}, u32[]{:S(2)}) %collective-permute-start.4) | collective-permute-done | bytes 32800 | tf_op jit(solution)/shard_map/while/body/eval_jaxpr/ppermute | solution.py:9
  50.2 0.7 collective-permute-start.1
  50.9 1.4 %collective-permute-start.3 = (f32[8,8]{1,0:T(8,128)S(1)}, f32[8,8]{1,0:T(8,128)S(1)}, u32[]{:S(2)}, u32[]{:S(2)}) collective-permute-start(f32[8,8]{1,0:T(8,128)S(1)} %copy.80), channel_id=1, source_target_pairs={{0,4},{4,8},{8,12},{12,16},{16,20},{20,24},{24,28},{28,0},{1,5},{5... | collective-permute-start | bytes 776 | tf_op jit(solution)/shard_map/while/body/eval_jaxpr/ppermute | solution.py:9
  52.8 0.7 copy-done.1
  54.0 0.3 fusion.74
  54.3 0.3 fusion.73
  54.9 3.3 %collective-permute-done.4 = f32[8,8,128]{2,1,0:T(8,128)S(1)} collective-permute-done((f32[8,8,128]{2,1,0:T(8,128)S(1)}, f32[8,8,128]{2,1,0:T(8,128)S(1)}, u32[]{:S(2)}, u32[]{:S(2)}) %collective-permute-start.4) | collective-permute-done | bytes 32800 | tf_op jit(solution)/shard_map/while/body/eval_jaxpr/ppermute | solution.py:9
  58.3 3.1 %collective-permute-start.3 = (f32[8,8]{1,0:T(8,128)S(1)}, f32[8,8]{1,0:T(8,128)S(1)}, u32[]{:S(2)}, u32[]{:S(2)}) collective-permute-start(f32[8,8]{1,0:T(8,128)S(1)} %copy.80), channel_id=1, source_target_pairs={{0,4},{4,8},{8,12},{12,16},{16,20},{20,24},{24,28},{28,0},{1,5},{5... | collective-permute-start | bytes 776 | tf_op jit(solution)/shard_map/while/body/eval_jaxpr/ppermute | solution.py:9
  61.6 0.2 fusion.70
  61.8 0.7 copy-done.1
  63.0 0.3 fusion.74
  63.4 0.3 fusion.73
  63.7 3.5 %collective-permute-done.4 = f32[8,8,128]{2,1,0:T(8,128)S(1)} collective-permute-done((f32[8,8,128]{2,1,0:T(8,128)S(1)}, f32[8,8,128]{2,1,0:T(8,128)S(1)}, u32[]{:S(2)}, u32[]{:S(2)}) %collective-permute-start.4) | collective-permute-done | bytes 32800 | tf_op jit(solution)/shard_map/while/body/eval_jaxpr/ppermute | solution.py:9
  67.4 2.0 %collective-permute-start.3 = (f32[8,8]{1,0:T(8,128)S(1)}, f32[8,8]{1,0:T(8,128)S(1)}, u32[]{:S(2)}, u32[]{:S(2)}) collective-permute-start(f32[8,8]{1,0:T(8,128)S(1)} %copy.80), channel_id=1, source_target_pairs={{0,4},{4,8},{8,12},{12,16},{16,20},{20,24},{24,28},{28,0},{1,5},{5... | collective-permute-start | bytes 776 | tf_op jit(solution)/shard_map/while/body/eval_jaxpr/ppermute | solution.py:9
  69.6 0.2 fusion.70
  69.8 0.7 copy-done.1
  71.0 0.3 fusion.74
  71.4 0.3 fusion.73
  71.8 3.5 %collective-permute-done.4 = f32[8,8,128]{2,1,0:T(8,128)S(1)} collective-permute-done((f32[8,8,128]{2,1,0:T(8,128)S(1)}, f32[8,8,128]{2,1,0:T(8,128)S(1)}, u32[]{:S(2)}, u32[]{:S(2)}) %collective-permute-start.4) | collective-permute-done | bytes 32800 | tf_op jit(solution)/shard_map/while/body/eval_jaxpr/ppermute | solution.py:9
  75.4 3.1 %collective-permute-start.3 = (f32[8,8]{1,0:T(8,128)S(1)}, f32[8,8]{1,0:T(8,128)S(1)}, u32[]{:S(2)}, u32[]{:S(2)}) collective-permute-start(f32[8,8]{1,0:T(8,128)S(1)} %copy.80), channel_id=1, source_target_pairs={{0,4},{4,8},{8,12},{12,16},{16,20},{20,24},{24,28},{28,0},{1,5},{5... | collective-permute-start | bytes 776 | tf_op jit(solution)/shard_map/while/body/eval_jaxpr/ppermute | solution.py:9
  78.6 0.2 fusion.70
  78.8 0.7 copy-done.1
  80.1 0.3 fusion.74
  80.4 0.3 fusion.73
  80.8 3.5 %collective-permute-done.4 = f32[8,8,128]{2,1,0:T(8,128)S(1)} collective-permute-done((f32[8,8,128]{2,1,0:T(8,128)S(1)}, f32[8,8,128]{2,1,0:T(8,128)S(1)}, u32[]{:S(2)}, u32[]{:S(2)}) %collective-permute-start.4) | collective-permute-done | bytes 32800 | tf_op jit(solution)/shard_map/while/body/eval_jaxpr/ppermute | solution.py:9
  84.4 2.0 %collective-permute-start.3 = (f32[8,8]{1,0:T(8,128)S(1)}, f32[8,8]{1,0:T(8,128)S(1)}, u32[]{:S(2)}, u32[]{:S(2)}) collective-permute-start(f32[8,8]{1,0:T(8,128)S(1)} %copy.80), channel_id=1, source_target_pairs={{0,4},{4,8},{8,12},{12,16},{16,20},{20,24},{24,28},{28,0},{1,5},{5... | collective-permute-start | bytes 776 | tf_op jit(solution)/shard_map/while/body/eval_jaxpr/ppermute | solution.py:9
  86.8 0.7 copy-done.1
  88.1 0.3 fusion.74
  88.4 0.3 fusion.73
  88.8 3.5 %collective-permute-done.4 = f32[8,8,128]{2,1,0:T(8,128)S(1)} collective-permute-done((f32[8,8,128]{2,1,0:T(8,128)S(1)}, f32[8,8,128]{2,1,0:T(8,128)S(1)}, u32[]{:S(2)}, u32[]{:S(2)}) %collective-permute-start.4) | collective-permute-done | bytes 32800 | tf_op jit(solution)/shard_map/while/body/eval_jaxpr/ppermute | solution.py:9
  92.4 3.1 %collective-permute-start.3 = (f32[8,8]{1,0:T(8,128)S(1)}, f32[8,8]{1,0:T(8,128)S(1)}, u32[]{:S(2)}, u32[]{:S(2)}) collective-permute-start(f32[8,8]{1,0:T(8,128)S(1)} %copy.80), channel_id=1, source_target_pairs={{0,4},{4,8},{8,12},{12,16},{16,20},{20,24},{24,28},{28,0},{1,5},{5... | collective-permute-start | bytes 776 | tf_op jit(solution)/shard_map/while/body/eval_jaxpr/ppermute | solution.py:9
  95.9 0.7 copy-done.1
  97.1 0.3 fusion.74
  97.4 0.3 fusion.73
  97.8 3.5 %collective-permute-done.4 = f32[8,8,128]{2,1,0:T(8,128)S(1)} collective-permute-done((f32[8,8,128]{2,1,0:T(8,128)S(1)}, f32[8,8,128]{2,1,0:T(8,128)S(1)}, u32[]{:S(2)}, u32[]{:S(2)}) %collective-permute-start.4) | collective-permute-done | bytes 32800 | tf_op jit(solution)/shard_map/while/body/eval_jaxpr/ppermute | solution.py:9
  101.5 0.7 copy-done.2
  102.7 1.0 fusion.24
  103.7 3.2 %collective-permute-done.5 = bf16[8,8,128]{2,1,0:T(8,128)(2,1)} collective-permute-done((bf16[8,8,128]{2,1,0:T(8,128)(2,1)S(1)}, bf16[8,8,128]{2,1,0:T(8,128)(2,1)}, u32[]{:S(2)}, u32[]{:S(2)}) %collective-permute-start.5) | collective-permute-done | bytes 16416 | tf_op jit(solution)/shard_map/ppermute | solution.py:9
  106.9 3.2 %all-to-all-start.4 = ((bf16[8,8,128]{2,1,0:T(8,128)(2,1)}), bf16[8,8,128]{2,1,0:T(8,128)(2,1)S(1)}, u32[]{:S(2)}, u32[]{:S(2)}) async-start(bf16[8,8,128]{2,1,0:T(8,128)(2,1)} %collective-permute-done.5), calls=%async_computation.4 | async-start | bytes 32768 | tf_op jit(solution)/shard_map/all_to_all | solution.py:99
  110.1 1.0 fusion.29
  111.1 4.6 %all-to-all-done.4 = bf16[8,8,128]{2,1,0:T(8,128)(2,1)S(1)} async-done(((bf16[8,8,128]{2,1,0:T(8,128)(2,1)}), bf16[8,8,128]{2,1,0:T(8,128)(2,1)S(1)}, u32[]{:S(2)}, u32[]{:S(2)}) %all-to-all-start.4) | async-done | bytes 16416 | tf_op jit(solution)/shard_map/all_to_all | solution.py:99
  115.7 0.6 copy.59
  (154 shorter events, 7.5 us)
Async XLA Ops:
  0.6 7.8 %copy-start.3 = (bf16[2,32,128]{2,1,0:T(8,128)(2,1)S(1)}, bf16[2,32,128]{2,1,0:T(8,128)(2,1)}, u32[]{:S(2)}) copy-start(bf16[2,32,128]{2,1,0:T(8,128)(2,1)} %param.9) | copy-start | bytes 49156
  0.6 39.8 %copy-start = (bf16[1024,1,128]{2,0,1:T(8,128)(2,1)S(1)}, bf16[1024,1,128]{2,0,1:T(8,128)(2,1)}, u32[]{:S(2)}) copy-start(bf16[1024,1,128]{2,0,1:T(8,128)(2,1)} %param.14) | copy-start | bytes 786436
  2.1 11.9 %all-to-all-start.2 = ((f32[2,4,8]{2,0,1:T(2,128)}), f32[2,4,8]{2,0,1:T(2,128)S(1)}, u32[]{:S(2)}, u32[]{:S(2)}) async-start(f32[2,4,8]{2,0,1:T(2,128)} %copy.31), calls=%async_computation.2 | async-start | bytes 8192 | tf_op jit(solution)/shard_map/all_to_all | solution.py:22
  14.0 8.8 %all-to-all-start = ((bf16[2,32,128]{2,0,1:T(2,128)(2,1)}), bf16[2,32,128]{2,0,1:T(2,128)(2,1)S(1)}, u32[]{:S(2)}, u32[]{:S(2)}) async-start(bf16[2,32,128]{2,0,1:T(2,128)(2,1)} %copy.27), calls=%async_computation | async-start | bytes 32768 | tf_op jit(solution)/shard_map/all_to_all | solution.py:18
  22.8 8.8 %all-to-all-start.1 = ((bf16[2,32,128]{2,0,1:T(2,128)(2,1)}), bf16[2,32,128]{2,0,1:T(2,128)(2,1)S(1)}, u32[]{:S(2)}, u32[]{:S(2)}) async-start(bf16[2,32,128]{2,0,1:T(2,128)(2,1)} %copy.29), calls=%async_computation.1 | async-start | bytes 32768 | tf_op jit(solution)/shard_map/all_to_all | solution.py:19
  31.7 8.8 %all-to-all-start.3 = ((f32[2,4,8]{2,0,1:T(2,128)}), f32[2,4,8]{2,0,1:T(2,128)S(1)}, u32[]{:S(2)}, u32[]{:S(2)}) async-start(f32[2,4,8]{2,0,1:T(2,128)} %copy.32), calls=%async_computation.3 | async-start | bytes 8192 | tf_op jit(solution)/shard_map/all_to_all | solution.py:23
  40.5 0.7 copy-start.4
  41.1 5.6 %collective-permute-start = (bf16[8,8,128]{2,0,1:T(8,128)(2,1)S(1)}, bf16[8,8,128]{2,0,1:T(8,128)(2,1)S(1)}, u32[]{:S(2)}, u32[]{:S(2)}) collective-permute-start(bf16[8,8,128]{2,0,1:T(8,128)(2,1)S(1)} %copy.77), channel_id=1, source_target_pairs={{0,4},{4,8},{8,12},{12,16},{16,20},{20,24},{24,28},{28,0},{1,5},{5... | collective-permute-start | bytes 49160 | tf_op jit(solution)/shard_map/while/body/eval_jaxpr/ppermute | solution.py:9
  41.1 5.6 %collective-permute-start.1 = (bf16[8,8,128]{2,0,1:T(8,128)(2,1)S(1)}, bf16[8,8,128]{2,0,1:T(8,128)(2,1)S(1)}, u32[]{:S(2)}, u32[]{:S(2)}) collective-permute-start(bf16[8,8,128]{2,0,1:T(8,128)(2,1)S(1)} %copy.78), channel_id=1, source_target_pairs={{0,4},{4,8},{8,12},{12,16},{16,20},{20,24},{24,28},{28,0},{1,5},{5... | collective-permute-start | bytes 49160 | tf_op jit(solution)/shard_map/while/body/eval_jaxpr/ppermute | solution.py:9
  42.7 3.9 %collective-permute-start.2 = (f32[8,8]{1,0:T(8,128)S(1)}, f32[8,8]{1,0:T(8,128)S(1)}, u32[]{:S(2)}, u32[]{:S(2)}) collective-permute-start(f32[8,8]{1,0:T(8,128)S(1)} %copy.79), channel_id=1, source_target_pairs={{0,4},{4,8},{8,12},{12,16},{16,20},{20,24},{24,28},{28,0},{1,5},{5... | collective-permute-start | bytes 776 | tf_op jit(solution)/shard_map/while/body/eval_jaxpr/ppermute | solution.py:9
  42.8 3.9 %collective-permute-start.3 = (f32[8,8]{1,0:T(8,128)S(1)}, f32[8,8]{1,0:T(8,128)S(1)}, u32[]{:S(2)}, u32[]{:S(2)}) collective-permute-start(f32[8,8]{1,0:T(8,128)S(1)} %copy.80), channel_id=1, source_target_pairs={{0,4},{4,8},{8,12},{12,16},{16,20},{20,24},{24,28},{28,0},{1,5},{5... | collective-permute-start | bytes 776 | tf_op jit(solution)/shard_map/while/body/eval_jaxpr/ppermute | solution.py:9
  44.5 1.0 copy-start.1
  45.9 4.3 %collective-permute-start.4 = (f32[8,8,128]{2,1,0:T(8,128)S(1)}, f32[8,8,128]{2,1,0:T(8,128)S(1)}, u32[]{:S(2)}, u32[]{:S(2)}) collective-permute-start(f32[8,8,128]{2,1,0:T(8,128)S(1)} %fusion.72), channel_id=1, source_target_pairs={{0,4},{4,8},{8,12},{12,16},{16,20},{20,24},{24,28},{28,0},{1,5},{5... | collective-permute-start | bytes 98312 | tf_op jit(solution)/shard_map/while/body/eval_jaxpr/ppermute | solution.py:9
  50.2 4.7 %collective-permute-start = (bf16[8,8,128]{2,0,1:T(8,128)(2,1)S(1)}, bf16[8,8,128]{2,0,1:T(8,128)(2,1)S(1)}, u32[]{:S(2)}, u32[]{:S(2)}) collective-permute-start(bf16[8,8,128]{2,0,1:T(8,128)(2,1)S(1)} %copy.77), channel_id=1, source_target_pairs={{0,4},{4,8},{8,12},{12,16},{16,20},{20,24},{24,28},{28,0},{1,5},{5... | collective-permute-start | bytes 49160 | tf_op jit(solution)/shard_map/while/body/eval_jaxpr/ppermute | solution.py:9
  50.2 4.7 %collective-permute-start.1 = (bf16[8,8,128]{2,0,1:T(8,128)(2,1)S(1)}, bf16[8,8,128]{2,0,1:T(8,128)(2,1)S(1)}, u32[]{:S(2)}, u32[]{:S(2)}) collective-permute-start(bf16[8,8,128]{2,0,1:T(8,128)(2,1)S(1)} %copy.78), channel_id=1, source_target_pairs={{0,4},{4,8},{8,12},{12,16},{16,20},{20,24},{24,28},{28,0},{1,5},{5... | collective-permute-start | bytes 49160 | tf_op jit(solution)/shard_map/while/body/eval_jaxpr/ppermute | solution.py:9
  50.9 3.9 %collective-permute-start.2 = (f32[8,8]{1,0:T(8,128)S(1)}, f32[8,8]{1,0:T(8,128)S(1)}, u32[]{:S(2)}, u32[]{:S(2)}) collective-permute-start(f32[8,8]{1,0:T(8,128)S(1)} %copy.79), channel_id=1, source_target_pairs={{0,4},{4,8},{8,12},{12,16},{16,20},{20,24},{24,28},{28,0},{1,5},{5... | collective-permute-start | bytes 776 | tf_op jit(solution)/shard_map/while/body/eval_jaxpr/ppermute | solution.py:9
  50.9 3.9 %collective-permute-start.3 = (f32[8,8]{1,0:T(8,128)S(1)}, f32[8,8]{1,0:T(8,128)S(1)}, u32[]{:S(2)}, u32[]{:S(2)}) collective-permute-start(f32[8,8]{1,0:T(8,128)S(1)} %copy.80), channel_id=1, source_target_pairs={{0,4},{4,8},{8,12},{12,16},{16,20},{20,24},{24,28},{28,0},{1,5},{5... | collective-permute-start | bytes 776 | tf_op jit(solution)/shard_map/while/body/eval_jaxpr/ppermute | solution.py:9
  52.5 1.0 copy-start.1
  53.9 4.3 %collective-permute-start.4 = (f32[8,8,128]{2,1,0:T(8,128)S(1)}, f32[8,8,128]{2,1,0:T(8,128)S(1)}, u32[]{:S(2)}, u32[]{:S(2)}) collective-permute-start(f32[8,8,128]{2,1,0:T(8,128)S(1)} %fusion.72), channel_id=1, source_target_pairs={{0,4},{4,8},{8,12},{12,16},{16,20},{20,24},{24,28},{28,0},{1,5},{5... | collective-permute-start | bytes 98312 | tf_op jit(solution)/shard_map/while/body/eval_jaxpr/ppermute | solution.py:9
  58.2 5.6 %collective-permute-start = (bf16[8,8,128]{2,0,1:T(8,128)(2,1)S(1)}, bf16[8,8,128]{2,0,1:T(8,128)(2,1)S(1)}, u32[]{:S(2)}, u32[]{:S(2)}) collective-permute-start(bf16[8,8,128]{2,0,1:T(8,128)(2,1)S(1)} %copy.77), channel_id=1, source_target_pairs={{0,4},{4,8},{8,12},{12,16},{16,20},{20,24},{24,28},{28,0},{1,5},{5... | collective-permute-start | bytes 49160 | tf_op jit(solution)/shard_map/while/body/eval_jaxpr/ppermute | solution.py:9
  58.2 5.6 %collective-permute-start.1 = (bf16[8,8,128]{2,0,1:T(8,128)(2,1)S(1)}, bf16[8,8,128]{2,0,1:T(8,128)(2,1)S(1)}, u32[]{:S(2)}, u32[]{:S(2)}) collective-permute-start(bf16[8,8,128]{2,0,1:T(8,128)(2,1)S(1)} %copy.78), channel_id=1, source_target_pairs={{0,4},{4,8},{8,12},{12,16},{16,20},{20,24},{24,28},{28,0},{1,5},{5... | collective-permute-start | bytes 49160 | tf_op jit(solution)/shard_map/while/body/eval_jaxpr/ppermute | solution.py:9
  58.3 5.4 %collective-permute-start.2 = (f32[8,8]{1,0:T(8,128)S(1)}, f32[8,8]{1,0:T(8,128)S(1)}, u32[]{:S(2)}, u32[]{:S(2)}) collective-permute-start(f32[8,8]{1,0:T(8,128)S(1)} %copy.79), channel_id=1, source_target_pairs={{0,4},{4,8},{8,12},{12,16},{16,20},{20,24},{24,28},{28,0},{1,5},{5... | collective-permute-start | bytes 776 | tf_op jit(solution)/shard_map/while/body/eval_jaxpr/ppermute | solution.py:9
  58.3 5.4 %collective-permute-start.3 = (f32[8,8]{1,0:T(8,128)S(1)}, f32[8,8]{1,0:T(8,128)S(1)}, u32[]{:S(2)}, u32[]{:S(2)}) collective-permute-start(f32[8,8]{1,0:T(8,128)S(1)} %copy.80), channel_id=1, source_target_pairs={{0,4},{4,8},{8,12},{12,16},{16,20},{20,24},{24,28},{28,0},{1,5},{5... | collective-permute-start | bytes 776 | tf_op jit(solution)/shard_map/while/body/eval_jaxpr/ppermute | solution.py:9
  61.6 1.0 copy-start.1
  62.9 4.3 %collective-permute-start.4 = (f32[8,8,128]{2,1,0:T(8,128)S(1)}, f32[8,8,128]{2,1,0:T(8,128)S(1)}, u32[]{:S(2)}, u32[]{:S(2)}) collective-permute-start(f32[8,8,128]{2,1,0:T(8,128)S(1)} %fusion.72), channel_id=1, source_target_pairs={{0,4},{4,8},{8,12},{12,16},{16,20},{20,24},{24,28},{28,0},{1,5},{5... | collective-permute-start | bytes 98312 | tf_op jit(solution)/shard_map/while/body/eval_jaxpr/ppermute | solution.py:9
  67.2 4.5 %collective-permute-start = (bf16[8,8,128]{2,0,1:T(8,128)(2,1)S(1)}, bf16[8,8,128]{2,0,1:T(8,128)(2,1)S(1)}, u32[]{:S(2)}, u32[]{:S(2)}) collective-permute-start(bf16[8,8,128]{2,0,1:T(8,128)(2,1)S(1)} %copy.77), channel_id=1, source_target_pairs={{0,4},{4,8},{8,12},{12,16},{16,20},{20,24},{24,28},{28,0},{1,5},{5... | collective-permute-start | bytes 49160 | tf_op jit(solution)/shard_map/while/body/eval_jaxpr/ppermute | solution.py:9
  67.2 4.5 %collective-permute-start.1 = (bf16[8,8,128]{2,0,1:T(8,128)(2,1)S(1)}, bf16[8,8,128]{2,0,1:T(8,128)(2,1)S(1)}, u32[]{:S(2)}, u32[]{:S(2)}) collective-permute-start(bf16[8,8,128]{2,0,1:T(8,128)(2,1)S(1)} %copy.78), channel_id=1, source_target_pairs={{0,4},{4,8},{8,12},{12,16},{16,20},{20,24},{24,28},{28,0},{1,5},{5... | collective-permute-start | bytes 49160 | tf_op jit(solution)/shard_map/while/body/eval_jaxpr/ppermute | solution.py:9
  67.3 4.4 %collective-permute-start.2 = (f32[8,8]{1,0:T(8,128)S(1)}, f32[8,8]{1,0:T(8,128)S(1)}, u32[]{:S(2)}, u32[]{:S(2)}) collective-permute-start(f32[8,8]{1,0:T(8,128)S(1)} %copy.79), channel_id=1, source_target_pairs={{0,4},{4,8},{8,12},{12,16},{16,20},{20,24},{24,28},{28,0},{1,5},{5... | collective-permute-start | bytes 776 | tf_op jit(solution)/shard_map/while/body/eval_jaxpr/ppermute | solution.py:9
  67.4 4.4 %collective-permute-start.3 = (f32[8,8]{1,0:T(8,128)S(1)}, f32[8,8]{1,0:T(8,128)S(1)}, u32[]{:S(2)}, u32[]{:S(2)}) collective-permute-start(f32[8,8]{1,0:T(8,128)S(1)} %copy.80), channel_id=1, source_target_pairs={{0,4},{4,8},{8,12},{12,16},{16,20},{20,24},{24,28},{28,0},{1,5},{5... | collective-permute-start | bytes 776 | tf_op jit(solution)/shard_map/while/body/eval_jaxpr/ppermute | solution.py:9
  69.6 1.0 copy-start.1
  70.9 4.3 %collective-permute-start.4 = (f32[8,8,128]{2,1,0:T(8,128)S(1)}, f32[8,8,128]{2,1,0:T(8,128)S(1)}, u32[]{:S(2)}, u32[]{:S(2)}) collective-permute-start(f32[8,8,128]{2,1,0:T(8,128)S(1)} %fusion.72), channel_id=1, source_target_pairs={{0,4},{4,8},{8,12},{12,16},{16,20},{20,24},{24,28},{28,0},{1,5},{5... | collective-permute-start | bytes 98312 | tf_op jit(solution)/shard_map/while/body/eval_jaxpr/ppermute | solution.py:9
  75.2 5.6 %collective-permute-start = (bf16[8,8,128]{2,0,1:T(8,128)(2,1)S(1)}, bf16[8,8,128]{2,0,1:T(8,128)(2,1)S(1)}, u32[]{:S(2)}, u32[]{:S(2)}) collective-permute-start(bf16[8,8,128]{2,0,1:T(8,128)(2,1)S(1)} %copy.77), channel_id=1, source_target_pairs={{0,4},{4,8},{8,12},{12,16},{16,20},{20,24},{24,28},{28,0},{1,5},{5... | collective-permute-start | bytes 49160 | tf_op jit(solution)/shard_map/while/body/eval_jaxpr/ppermute | solution.py:9
  75.2 5.6 %collective-permute-start.1 = (bf16[8,8,128]{2,0,1:T(8,128)(2,1)S(1)}, bf16[8,8,128]{2,0,1:T(8,128)(2,1)S(1)}, u32[]{:S(2)}, u32[]{:S(2)}) collective-permute-start(bf16[8,8,128]{2,0,1:T(8,128)(2,1)S(1)} %copy.78), channel_id=1, source_target_pairs={{0,4},{4,8},{8,12},{12,16},{16,20},{20,24},{24,28},{28,0},{1,5},{5... | collective-permute-start | bytes 49160 | tf_op jit(solution)/shard_map/while/body/eval_jaxpr/ppermute | solution.py:9
  75.3 5.4 %collective-permute-start.2 = (f32[8,8]{1,0:T(8,128)S(1)}, f32[8,8]{1,0:T(8,128)S(1)}, u32[]{:S(2)}, u32[]{:S(2)}) collective-permute-start(f32[8,8]{1,0:T(8,128)S(1)} %copy.79), channel_id=1, source_target_pairs={{0,4},{4,8},{8,12},{12,16},{16,20},{20,24},{24,28},{28,0},{1,5},{5... | collective-permute-start | bytes 776 | tf_op jit(solution)/shard_map/while/body/eval_jaxpr/ppermute | solution.py:9
  75.4 5.4 %collective-permute-start.3 = (f32[8,8]{1,0:T(8,128)S(1)}, f32[8,8]{1,0:T(8,128)S(1)}, u32[]{:S(2)}, u32[]{:S(2)}) collective-permute-start(f32[8,8]{1,0:T(8,128)S(1)} %copy.80), channel_id=1, source_target_pairs={{0,4},{4,8},{8,12},{12,16},{16,20},{20,24},{24,28},{28,0},{1,5},{5... | collective-permute-start | bytes 776 | tf_op jit(solution)/shard_map/while/body/eval_jaxpr/ppermute | solution.py:9
  78.6 1.0 copy-start.1
  79.9 4.3 %collective-permute-start.4 = (f32[8,8,128]{2,1,0:T(8,128)S(1)}, f32[8,8,128]{2,1,0:T(8,128)S(1)}, u32[]{:S(2)}, u32[]{:S(2)}) collective-permute-start(f32[8,8,128]{2,1,0:T(8,128)S(1)} %fusion.72), channel_id=1, source_target_pairs={{0,4},{4,8},{8,12},{12,16},{16,20},{20,24},{24,28},{28,0},{1,5},{5... | collective-permute-start | bytes 98312 | tf_op jit(solution)/shard_map/while/body/eval_jaxpr/ppermute | solution.py:9
  84.2 4.5 %collective-permute-start = (bf16[8,8,128]{2,0,1:T(8,128)(2,1)S(1)}, bf16[8,8,128]{2,0,1:T(8,128)(2,1)S(1)}, u32[]{:S(2)}, u32[]{:S(2)}) collective-permute-start(bf16[8,8,128]{2,0,1:T(8,128)(2,1)S(1)} %copy.77), channel_id=1, source_target_pairs={{0,4},{4,8},{8,12},{12,16},{16,20},{20,24},{24,28},{28,0},{1,5},{5... | collective-permute-start | bytes 49160 | tf_op jit(solution)/shard_map/while/body/eval_jaxpr/ppermute | solution.py:9
  84.2 4.5 %collective-permute-start.1 = (bf16[8,8,128]{2,0,1:T(8,128)(2,1)S(1)}, bf16[8,8,128]{2,0,1:T(8,128)(2,1)S(1)}, u32[]{:S(2)}, u32[]{:S(2)}) collective-permute-start(bf16[8,8,128]{2,0,1:T(8,128)(2,1)S(1)} %copy.78), channel_id=1, source_target_pairs={{0,4},{4,8},{8,12},{12,16},{16,20},{20,24},{24,28},{28,0},{1,5},{5... | collective-permute-start | bytes 49160 | tf_op jit(solution)/shard_map/while/body/eval_jaxpr/ppermute | solution.py:9
  84.3 4.4 %collective-permute-start.2 = (f32[8,8]{1,0:T(8,128)S(1)}, f32[8,8]{1,0:T(8,128)S(1)}, u32[]{:S(2)}, u32[]{:S(2)}) collective-permute-start(f32[8,8]{1,0:T(8,128)S(1)} %copy.79), channel_id=1, source_target_pairs={{0,4},{4,8},{8,12},{12,16},{16,20},{20,24},{24,28},{28,0},{1,5},{5... | collective-permute-start | bytes 776 | tf_op jit(solution)/shard_map/while/body/eval_jaxpr/ppermute | solution.py:9
  84.4 4.4 %collective-permute-start.3 = (f32[8,8]{1,0:T(8,128)S(1)}, f32[8,8]{1,0:T(8,128)S(1)}, u32[]{:S(2)}, u32[]{:S(2)}) collective-permute-start(f32[8,8]{1,0:T(8,128)S(1)} %copy.80), channel_id=1, source_target_pairs={{0,4},{4,8},{8,12},{12,16},{16,20},{20,24},{24,28},{28,0},{1,5},{5... | collective-permute-start | bytes 776 | tf_op jit(solution)/shard_map/while/body/eval_jaxpr/ppermute | solution.py:9
  86.6 1.0 copy-start.1
  88.0 4.3 %collective-permute-start.4 = (f32[8,8,128]{2,1,0:T(8,128)S(1)}, f32[8,8,128]{2,1,0:T(8,128)S(1)}, u32[]{:S(2)}, u32[]{:S(2)}) collective-permute-start(f32[8,8,128]{2,1,0:T(8,128)S(1)} %fusion.72), channel_id=1, source_target_pairs={{0,4},{4,8},{8,12},{12,16},{16,20},{20,24},{24,28},{28,0},{1,5},{5... | collective-permute-start | bytes 98312 | tf_op jit(solution)/shard_map/while/body/eval_jaxpr/ppermute | solution.py:9
  92.3 5.6 %collective-permute-start = (bf16[8,8,128]{2,0,1:T(8,128)(2,1)S(1)}, bf16[8,8,128]{2,0,1:T(8,128)(2,1)S(1)}, u32[]{:S(2)}, u32[]{:S(2)}) collective-permute-start(bf16[8,8,128]{2,0,1:T(8,128)(2,1)S(1)} %copy.77), channel_id=1, source_target_pairs={{0,4},{4,8},{8,12},{12,16},{16,20},{20,24},{24,28},{28,0},{1,5},{5... | collective-permute-start | bytes 49160 | tf_op jit(solution)/shard_map/while/body/eval_jaxpr/ppermute | solution.py:9
  92.3 5.6 %collective-permute-start.1 = (bf16[8,8,128]{2,0,1:T(8,128)(2,1)S(1)}, bf16[8,8,128]{2,0,1:T(8,128)(2,1)S(1)}, u32[]{:S(2)}, u32[]{:S(2)}) collective-permute-start(bf16[8,8,128]{2,0,1:T(8,128)(2,1)S(1)} %copy.78), channel_id=1, source_target_pairs={{0,4},{4,8},{8,12},{12,16},{16,20},{20,24},{24,28},{28,0},{1,5},{5... | collective-permute-start | bytes 49160 | tf_op jit(solution)/shard_map/while/body/eval_jaxpr/ppermute | solution.py:9
  92.3 5.5 %collective-permute-start.2 = (f32[8,8]{1,0:T(8,128)S(1)}, f32[8,8]{1,0:T(8,128)S(1)}, u32[]{:S(2)}, u32[]{:S(2)}) collective-permute-start(f32[8,8]{1,0:T(8,128)S(1)} %copy.79), channel_id=1, source_target_pairs={{0,4},{4,8},{8,12},{12,16},{16,20},{20,24},{24,28},{28,0},{1,5},{5... | collective-permute-start | bytes 776 | tf_op jit(solution)/shard_map/while/body/eval_jaxpr/ppermute | solution.py:9
  92.4 5.4 %collective-permute-start.3 = (f32[8,8]{1,0:T(8,128)S(1)}, f32[8,8]{1,0:T(8,128)S(1)}, u32[]{:S(2)}, u32[]{:S(2)}) collective-permute-start(f32[8,8]{1,0:T(8,128)S(1)} %copy.80), channel_id=1, source_target_pairs={{0,4},{4,8},{8,12},{12,16},{16,20},{20,24},{24,28},{28,0},{1,5},{5... | collective-permute-start | bytes 776 | tf_op jit(solution)/shard_map/while/body/eval_jaxpr/ppermute | solution.py:9
  95.6 1.0 copy-start.1
  97.0 4.3 %collective-permute-start.4 = (f32[8,8,128]{2,1,0:T(8,128)S(1)}, f32[8,8,128]{2,1,0:T(8,128)S(1)}, u32[]{:S(2)}, u32[]{:S(2)}) collective-permute-start(f32[8,8,128]{2,1,0:T(8,128)S(1)} %fusion.72), channel_id=1, source_target_pairs={{0,4},{4,8},{8,12},{12,16},{16,20},{20,24},{24,28},{28,0},{1,5},{5... | collective-permute-start | bytes 98312 | tf_op jit(solution)/shard_map/while/body/eval_jaxpr/ppermute | solution.py:9
  101.3 1.0 copy-start.2
  102.6 4.2 %collective-permute-start.5 = (bf16[8,8,128]{2,1,0:T(8,128)(2,1)S(1)}, bf16[8,8,128]{2,1,0:T(8,128)(2,1)}, u32[]{:S(2)}, u32[]{:S(2)}) collective-permute-start(bf16[8,8,128]{2,1,0:T(8,128)(2,1)S(1)} %fusion.32), channel_id=1, source_target_pairs={{0,4},{4,8},{8,12},{12,16},{16,20},{20,24},{24,28},{28,0},{1,5},{5... | collective-permute-start | bytes 49160 | tf_op jit(solution)/shard_map/ppermute | solution.py:9
  106.9 8.8 %all-to-all-start.4 = ((bf16[8,8,128]{2,1,0:T(8,128)(2,1)}), bf16[8,8,128]{2,1,0:T(8,128)(2,1)S(1)}, u32[]{:S(2)}, u32[]{:S(2)}) async-start(bf16[8,8,128]{2,1,0:T(8,128)(2,1)} %collective-permute-done.5), calls=%async_computation.4 | async-start | bytes 32768 | tf_op jit(solution)/shard_map/all_to_all | solution.py:99
where the time goes:
time: 117 us; the launch traced here: 116 us
  waiting for transfers between devices  50 us (43%)
  starting transfers between devices  39.4 us (34%)
  local copies, waits for them, and re-layouts  12.4 us (11%)
  matrix products  11.5 us (10%)
  other arithmetic  1.51 us (1%)
    ppermute x36, waiting for transfers between devices, shifted(): lax.ppermute(value, axis, [(i, (i + by) % peers) for i in range(peers)])  27.5 us
    ppermute x36, starting transfers between devices, shifted(): lax.ppermute(value, axis, [(i, (i + by) % peers) for i in range(peers)])  20.1 us
    all_to_all x1, starting transfers between devices, local(): lax.all_to_all(log_norms, 'kvh', split_axis=1, concat_axis=0, tiled=True)  6.35 us
    all_to_all x1, waiting for transfers between devices, local(): lax.all_to_all(deltas, 'kvh', split_axis=1, concat_axis=0, tiled=True)  5.48 us
    while x42, local copies, waits for them, and re-layouts  5.07 us
    all_to_all x1, waiting for transfers between devices, local(): lax.all_to_all(query_grad.astype(jnp.bfloat16), 'kvh', split_axis=0, conc...  4.59 us
    all_to_all x1, waiting for transfers between devices, local(): lax.all_to_all(log_norms, 'kvh', split_axis=1, concat_axis=0, tiled=True)  4.21 us
    all_to_all x1, waiting for transfers between devices, local(): lax.all_to_all(queries, 'kvh', split_axis=1, concat_axis=0, tiled=True)  4.16 us
  transfers between devices with their start and end apart: 41, of which 16 were waited for; matrix products, arithmetic and copies ran while one was open for 14% of the time, Pallas kernels for 0%

commit v1 on v0

v1 whole, which is shorter than its diff:
```python
import functools
import math

import jax
import jax.numpy as jnp
from jax import lax
from jax.experimental import pallas as pl
from jax.experimental.pallas import tpu as pltpu
from jax.sharding import PartitionSpec as P

LANES = 128
PARTS = 3
BF = jnp.bfloat16
F32 = jnp.float32
VM = pl.BlockSpec(memory_space=pltpu.VMEM)


def split_parts(value):
    out = []
    for _ in range(PARTS):
        part = value.astype(BF)
        out.append(part)
        value = value - part.astype(F32)
    return out


def prep_body(q_ref, g_ref, o_ref, n_ref, out_ref, *, root):
    tokens, heads, _ = q_ref.shape
    seqs, kvs, rows, _ = out_ref.shape
    group = heads // kvs
    block = tokens * group
    stride = LANES // tokens
    lane = lax.broadcasted_iota(jnp.int32, (heads, LANES), 1)
    extra = jnp.zeros((heads, LANES), F32)
    pick = lax.broadcasted_iota(jnp.int32, (heads, heads), 0) == lax.broadcasted_iota(
        jnp.int32, (heads, heads), 1
    )
    for t in range(tokens):
        g = g_ref[t].astype(F32)
        o = o_ref[t].astype(F32)
        delta = jnp.sum(g * o, axis=-1, keepdims=True)
        norm_row = jnp.broadcast_to(n_ref[t : t + 1, :], (heads, heads))
        norm = jnp.sum(jnp.where(pick, norm_row, 0.0), axis=-1, keepdims=True) * root
        for p, part in enumerate(split_parts(norm) + split_parts(delta)):
            extra = jnp.where(lane == t * stride + p, part.astype(F32), extra)
    extra = extra.astype(BF)
    for k in range(kvs):
        part = slice(k * group, (k + 1) * group)
        for s in range(seqs):
            for t in range(tokens):
                out_ref[s, k, t * group : (t + 1) * group, :] = q_ref[t, part, :]
                out_ref[s, k, block + t * group : block + (t + 1) * group, :] = g_ref[t, part, :]
            out_ref[s, k, 2 * block : rows, :] = extra[part, :]


def unpack(m_ref, first, count, tokens, group):
    block = tokens * group
    stride = LANES // tokens
    q = m_ref[pl.ds(first, count), 0:block, :].reshape(count * block, LANES)
    g = m_ref[pl.ds(first, count), block : 2 * block, :].reshape(count * block, LANES)
    e = m_ref[pl.ds(first, count), 2 * block : 2 * block + group, :]
    lane = lax.broadcasted_iota(jnp.int32, (count, group, LANES), 2)
    pieces = [jnp.where((lane >= t * stride) & (lane < (t + 1) * stride), e, jnp.zeros_like(e)) for t in range(tokens)]
    extra = jnp.stack(pieces, axis=1).reshape(count * block, LANES)
    return q, g, extra


def grads_body(m_ref, k_ref, v_ref, lo_ref, hi_ref, w_ref, s_ref, dq_ref, *, tokens, group, step, scaling):
    messages = m_ref.shape[0]
    keys = k_ref.shape[0]
    block = tokens * group
    stride = LANES // tokens
    lane = lax.broadcasted_iota(jnp.int32, (keys, LANES), 1) % stride
    minus = jnp.full((keys, LANES), -1.0, F32)
    norm_cols = jnp.where(lane < PARTS, minus, 0.0).astype(BF)
    delta_cols = jnp.where((lane >= PARTS) & (lane < 2 * PARTS), minus, 0.0).astype(BF)
    k_wide = jnp.concatenate([k_ref[...], norm_cols], axis=1)
    v_wide = jnp.concatenate([v_ref[...], delta_cols], axis=1)
    factor = scaling * math.log2(math.e)
    nt = (((1,), (1,)), ((), ()))
    rows = step * block

    def visit(at):
        first = pl.ds(at * rows, rows)
        q, g, extra = unpack(m_ref, at * step, step, tokens, group)
        scores = lax.dot_general(jnp.concatenate([q, extra], axis=1), k_wide, nt, preferred_element_type=F32)
        pos = lax.broadcasted_iota(jnp.int32, (rows, keys), 1)
        lo = jnp.tile(lo_ref[first, :], (1, keys // LANES))
        hi = jnp.tile(hi_ref[first, :], (1, keys // LANES))
        weights = jnp.where((pos >= lo) & (pos <= hi), jnp.exp2(scores * factor), 0.0)
        pulled = lax.dot_general(jnp.concatenate([g, extra], axis=1), v_wide, nt, preferred_element_type=F32)
        s_half = (weights * pulled).astype(BF)
        w_ref[first, :] = weights.astype(BF)
        s_ref[first, :] = s_half
        dq = jnp.dot(s_half, k_ref[...], preferred_element_type=F32) * scaling
        dq_ref[pl.ds(at * step, step)] = dq.astype(BF).reshape(step, block, LANES)

    if messages // step <= 4:
        for at in range(messages // step):
            visit(at)
    else:

        @pl.loop(0, messages // step)
        def _(at):
            visit(at)


def context_body(m_ref, w_ref, s_ref, dk_ref, dv_ref, *, tokens, group, step, scaling):
    messages = m_ref.shape[0]
    block = tokens * group
    rows = step * block
    tn = (((0,), (0,)), ((), ()))
    keys = w_ref.shape[1]

    def visit(at, sums):
        first = pl.ds(at * rows, rows)
        q = m_ref[pl.ds(at * step, step), 0:block, :].reshape(rows, LANES)
        g = m_ref[pl.ds(at * step, step), block : 2 * block, :].reshape(rows, LANES)
        dk = lax.dot_general(s_ref[first, :], q, tn, preferred_element_type=F32)
        dv = lax.dot_general(w_ref[first, :], g, tn, preferred_element_type=F32)
        return (sums[0] + dk, sums[1] + dv)

    zero = jnp.zeros((keys, LANES), F32)
    if messages // step == 1:
        sums = visit(0, (zero, zero))
    else:
        sums = lax.fori_loop(0, messages // step, visit, (zero, zero))
    dk_ref[...] = (sums[0] * scaling).astype(BF)
    dv_ref[...] = sums[1].astype(BF)


def local(queries, attn_out, grad_out, log_norms, query_starts, keys, values):
    scaling = queries.shape[-1] ** (-0.5)
    seqs, kvs = lax.axis_size("seq"), lax.axis_size("kvh")
    peers = seqs * kvs
    tokens, heads, width = queries.shape
    group = heads // kvs
    block = tokens * group
    rows = peers * block
    both = ("seq", "kvh")
    message = pl.pallas_call(
        functools.partial(prep_body, root=1.0 / scaling),
        out_shape=jax.ShapeDtypeStruct((seqs, kvs, 2 * block + group, width), BF),
        in_specs=[VM] * 4,
        out_specs=VM,
        name="prep",
    )(queries, grad_out, attn_out, log_norms)
    message = message.reshape(peers, 2 * block + group, width)
    got = lax.all_to_all(message, both, split_axis=0, concat_axis=0, tiled=True)

    key_count = keys.shape[0]
    base = lax.axis_index("seq") * key_count
    all_tokens = query_starts.shape[0]
    last = seqs * key_count - all_tokens + jnp.arange(all_tokens, dtype=jnp.int32) - base
    spread = lambda x: jnp.broadcast_to(jnp.repeat(x, group)[:, None], (rows, LANES))
    lo, hi = spread(query_starts - base), spread(last)
    key_rows, value_rows = keys[:, 0, :], values[:, 0, :]
    step = min(peers, 8)
    weights, score_grads, partial = pl.pallas_call(
        functools.partial(grads_body, tokens=tokens, group=group, step=step, scaling=scaling),
        out_shape=(
            jax.ShapeDtypeStruct((rows, key_count), BF),
            jax.ShapeDtypeStruct((rows, key_count), BF),
            jax.ShapeDtypeStruct((peers, block, width), BF),
        ),
        in_specs=[VM] * 5,
        out_specs=(VM, VM, VM),
        name="grads",
    )(got, key_rows, value_rows, lo, hi)
    back = lax.all_to_all(partial, both, split_axis=0, concat_axis=0, tiled=True)
    grad_keys, grad_values = pl.pallas_call(
        functools.partial(context_body, tokens=tokens, group=group, step=min(peers, 32), scaling=scaling),
        out_shape=(jax.ShapeDtypeStruct((key_count, width), BF),) * 2,
        in_specs=[VM] * 3,
        out_specs=(VM, VM),
        name="context",
    )(got, weights, score_grads)
    back = back.reshape(seqs, kvs, tokens, group, width).astype(F32)
    grad_query = jnp.sum(back, axis=0).transpose(1, 0, 2, 3).reshape(tokens, heads, width).astype(BF)
    return (grad_query, grad_keys[:, None, :], grad_values[:, None, :])


def solution(mesh):
    return jax.shard_map(
        local,
        mesh=mesh,
        in_specs=(
            P(("seq", "kvh"), None, None),
            P(("seq", "kvh"), None, None),
            P(("seq", "kvh"), None, None),
            P(("seq", "kvh"), None),
            P(),
            P("seq", "kvh", None),
            P("seq", "kvh", None),
        ),
        out_specs=(P(("seq", "kvh"), None, None), P("seq", "kvh", None), P("seq", "kvh", None)),
        check_vma=False,
    )
```

time: 117 us -> 39.6 us (0.34)
  waiting for transfers between devices: 50 us -> 15.3 us
  starting transfers between devices: 39.4 us -> 10.5 us
  matrix products: 11.5 us -> 0 us
  Pallas kernels: 0 us -> 9.45 us
  local copies, waits for them, and re-layouts: 12.4 us -> 3.27 us
  other arithmetic: 1.51 us -> 0.03 us
    ppermute x36 -> x0, waiting for transfers between devices: 27.5 us -> none  [shifted(): lax.ppermute(value, axis, [(i, (i + by) % peers) for i in range(peers)])]
    ppermute x36 -> x0, starting transfers between devices: 20.1 us -> none  [shifted(): lax.ppermute(value, axis, [(i, (i + by) % peers) for i in range(peers)])]
    dot_general x40 -> x0, matrix products: 11.5 us -> none  [the longest x8 3.34 us: block_terms(): jnp.einsum('rgk,rgd->kd', score_half, queries_in, preferred_element_type=...]
    pallas_call x0 -> x3, Pallas kernels: none -> 9.45 us  [the longest x1 4.67 us: local(): pl.pallas_call(functools.partial(grads_body, tokens=tokens, group=group,...]
    all_to_all x5 -> x2, starting transfers between devices: 19.3 us -> 10.5 us  [the longest x1 7.33 us: local(): got = lax.all_to_all(message, both, split_axis=0, concat_axis=0, tiled=True)]
    all_to_all x5 -> x2, waiting for transfers between devices: 22.5 us -> 15.3 us  [the longest x1 10 us: local(): got = lax.all_to_all(message, both, split_axis=0, concat_axis=0, tiled=True)]
    while x42 -> x0, local copies, waits for them, and re-layouts: 5.07 us -> none
    all_to_all x7 -> x0, local copies, waits for them, and re-layouts: 2.73 us -> none  [the longest x2 1.4 us: local(): lax.all_to_all(log_norms, 'kvh', split_axis=1, concat_axis=0, tiled=True)]
  transfers between devices with their start and end apart: 41 -> 2, of which waited for: 16 -> 2; matrix products, arithmetic and copies ran while one was open for 14% -> 1% of each run, Pallas kernels for 0% -> 8%
where the time goes in v1:
time: 39.6 us; the launch traced here: 39.2 us
  waiting for transfers between devices  15.3 us (39%)
  starting transfers between devices  10.5 us (27%)
  Pallas kernels  9.45 us (24%)
  local copies, waits for them, and re-layouts  3.27 us (8%)
  between operations  0.67 us (2%)
    all_to_all x1, waiting for transfers between devices, local(): got = lax.all_to_all(message, both, split_axis=0, concat_axis=0, tiled=True)  10 us
    all_to_all x1, starting transfers between devices, local(): got = lax.all_to_all(message, both, split_axis=0, concat_axis=0, tiled=True)  7.33 us
    all_to_all x1, waiting for transfers between devices, local(): lax.all_to_all(partial, both, split_axis=0, concat_axis=0, tiled=True)  5.21 us
    pallas_call x1, Pallas kernels, local(): pl.pallas_call(functools.partial(grads_body, tokens=tokens, group=group,...  4.67 us
    all_to_all x1, starting transfers between devices, local(): lax.all_to_all(partial, both, split_axis=0, concat_axis=0, tiled=True)  3.21 us
    pallas_call x1, Pallas kernels, local(): pl.pallas_call(functools.partial(context_body, tokens=tokens, group=group...  3.17 us
    broadcast_in_dim x4, local copies, waits for them, and re-layouts, local(): jnp.broadcast_to(jnp.repeat(x, group)[:, None], (rows, LANES))  1.86 us
    pallas_call x1, Pallas kernels, local(): pl.pallas_call(functools.partial(prep_body, root=1.0 / scaling), out_shap...  1.61 us
  transfers between devices with their start and end apart: 2, of which 2 were waited for; matrix products, arithmetic and copies ran while one was open for 1% of the time, Pallas kernels for 8%

profile of v1, /device:TPU:0, one launch (start us, length us, event | category | flops | bytes accessed | tf_op | source)
XLA Modules:
  0.0 39.2 jit_solution(8834191013137529647)
XLA Ops:
  0.6 1.6 %prep.1 = bf16[8,4,40,128]{3,2,1,0:T(8,128)(2,1)} custom-call(bf16[2,32,128]{2,1,0:T(8,128)(2,1)} %q_ref.1, bf16[2,32,128]{2,1,0:T(8,128)(2,1)} %g_ref.1, bf16[2,32,128]{2,1,0:T(8,128)(2,1)} %o_ref.1, f32[2,32]{1,0:T(2,128)} %n_ref.1), custom_call_target="tpu_custom_call" | custom-call | tf_op jit(solution)/shard_map/prep/pallas_call | solution.py:141
  2.2 7.3 %all-to-all-start = ((bf16[32,40,128]{2,1,0:T(8,128)(2,1)}), bf16[32,40,128]{2,1,0:T(8,128)(2,1)S(1)}, u32[]{:S(2)}, u32[]{:S(2)}) async-start(bf16[32,40,128]{2,1,0:T(8,128)(2,1)} %bitcast.11), calls=%async_computation | async-start | bytes 655360 | tf_op jit(solution)/shard_map/all_to_all | solution.py:149
  9.6 0.0 copy-start.1
  9.6 0.6 %copy-done.1 = s32[64]{0:T(128)S(1)} copy-done((s32[64]{0:T(128)S(1)}, s32[64]{0:T(128)}, u32[]{:S(2)}) %copy-start.1) | copy-done | bytes 280
  10.2 0.1 broadcast_in_dim.29
  10.3 0.1 broadcast_in_dim.30
  10.4 0.1 broadcast_in_dim.26
  10.5 0.1 broadcast_in_dim.27
  10.6 10.0 %all-to-all-done.m_ref = bf16[32,40,128]{2,1,0:T(8,128)(2,1)S(1)} async-done(((bf16[32,40,128]{2,1,0:T(8,128)(2,1)}), bf16[32,40,128]{2,1,0:T(8,128)(2,1)S(1)}, u32[]{:S(2)}, u32[]{:S(2)}) %all-to-all-start) | async-done | bytes 327712 | tf_op jit(solution)/shard_map/all_to_all | solution.py:149
  20.6 0.0 copy-start
  20.6 0.8 %broadcast_in_dim.28.lo_ref = s32[512,128]{1,0:T(8,128)} broadcast(s32[512]{0:T(512)S(1)} %broadcast_in_dim.27), dimensions={0} | broadcast | bytes 264192 | tf_op jit(solution)/shard_map/broadcast_in_dim | solution.py:155
  21.5 0.8 %broadcast_in_dim.31.hi_ref = s32[512,128]{1,0:T(8,128)} broadcast(s32[512]{0:T(512)S(1)} %broadcast_in_dim.30), dimensions={0} | broadcast | bytes 264192 | tf_op jit(solution)/shard_map/broadcast_in_dim | solution.py:155
  22.3 0.0 copy-done
  22.3 4.7 %grads.1 = (bf16[512,1024]{1,0:T(8,128)(2,1)}, bf16[512,1024]{1,0:T(8,128)(2,1)}, bf16[32,16,128]{2,1,0:T(8,128)(2,1)}) custom-call(bf16[32,40,128]{2,1,0:T(8,128)(2,1)} %copy-done, bf16[1024,128]{1,0:T(8,128)(2,1)} %bitcast.13, bf16[1024,128]{1,0:T(8,128)(2,1)} %bitcast.14, s32[512,128]{1,0:T(8,128)} %broadcast_in_dim.28.lo_ref, ...), custom_call_target="tpu_custom_call" | custom-call | tf_op jit(solution)/shard_map/grads/pallas_call | solution.py:159
  27.0 3.2 %all-to-all-start.1 = ((bf16[32,16,128]{2,1,0:T(8,128)(2,1)}), bf16[32,16,128]{2,1,0:T(8,128)(2,1)S(1)}, u32[]{:S(2)}, u32[]{:S(2)}) async-start(bf16[32,16,128]{2,1,0:T(8,128)(2,1)} %get-tuple-element.8), calls=%async_computation.1 | async-start | bytes 262144 | tf_op jit(solution)/shard_map/all_to_all | solution.py:170
  30.2 3.2 %context.1 = (bf16[1024,128]{1,0:T(8,128)(2,1)}, bf16[1024,128]{1,0:T(8,128)(2,1)}) custom-call(bf16[32,40,128]{2,1,0:T(8,128)(2,1)} %copy-done, bf16[512,1024]{1,0:T(8,128)(2,1)} %get-tuple-element.9.w_ref, bf16[512,1024]{1,0:T(8,128)(2,1)} %get-tuple-element.10.s_ref), custom_call_target="tpu_custom_call" | custom-call | tf_op jit(solution)/shard_map/context/pallas_call | solution.py:171
  33.4 5.2 %all-to-all-done.1 = bf16[32,16,128]{2,1,0:T(8,128)(2,1)S(1)} async-done(((bf16[32,16,128]{2,1,0:T(8,128)(2,1)}), bf16[32,16,128]{2,1,0:T(8,128)(2,1)S(1)}, u32[]{:S(2)}, u32[]{:S(2)}) %all-to-all-start.1) | async-done | bytes 131104 | tf_op jit(solution)/shard_map/all_to_all | solution.py:170
  38.6 0.6 %copy_bitcast_fusion = bf16[2,32,128]{2,1,0:T(8,128)(2,1)} fusion(bf16[4,2,8,128]{3,2,1,0:T(8,128)(2,1)S(1)} %reduce), kind=kLoop, calls=%fused_computation | loop fusion | bytes 32768 | tf_op jit(solution)/shard_map/convert_element_type | solution.py:179
  (2 shorter events, 0.0 us)
Async XLA Ops:
  2.2 18.4 %all-to-all-start = ((bf16[32,40,128]{2,1,0:T(8,128)(2,1)}), bf16[32,40,128]{2,1,0:T(8,128)(2,1)S(1)}, u32[]{:S(2)}, u32[]{:S(2)}) async-start(bf16[32,40,128]{2,1,0:T(8,128)(2,1)} %bitcast.11), calls=%async_computation | async-start | bytes 655360 | tf_op jit(solution)/shard_map/all_to_all | solution.py:149
  9.6 0.7 %copy-start.1 = (s32[64]{0:T(128)S(1)}, s32[64]{0:T(128)}, u32[]{:S(2)}) copy-start(s32[64]{0:T(128)} %param.11) | copy-start | bytes 772
  20.6 1.7 %copy-start = (bf16[32,40,128]{2,1,0:T(8,128)(2,1)}, bf16[32,40,128]{2,1,0:T(8,128)(2,1)S(1)}, u32[]{:S(2)}) copy-start(bf16[32,40,128]{2,1,0:T(8,128)(2,1)S(1)} %all-to-all-done.m_ref) | copy-start | bytes 983044
  27.0 11.6 %all-to-all-start.1 = ((bf16[32,16,128]{2,1,0:T(8,128)(2,1)}), bf16[32,16,128]{2,1,0:T(8,128)(2,1)S(1)}, u32[]{:S(2)}, u32[]{:S(2)}) async-start(bf16[32,16,128]{2,1,0:T(8,128)(2,1)} %get-tuple-element.8), calls=%async_computation.1 | async-start | bytes 262144 | tf_op jit(solution)/shard_map/all_to_all | solution.py:170

commit v2 on v1

v2 whole, which is shorter than its diff:
```python
import functools
import math

import jax
import jax.numpy as jnp
from jax import lax
from jax.experimental import pallas as pl
from jax.experimental.pallas import tpu as pltpu
from jax.sharding import PartitionSpec as P

LANES = 128
PARTS = 3
BF = jnp.bfloat16
F32 = jnp.float32
VM = pl.BlockSpec(memory_space=pltpu.VMEM)
ANY = pl.BlockSpec(memory_space=pl.ANY)


SMALL = 1 << 20


def held(shape, dtype=BF):
    if math.prod(shape) * jnp.dtype(dtype).itemsize <= SMALL:
        return pltpu.VMEM(shape, dtype)
    return jax.ShapeDtypeStruct(shape, dtype)


def fast(value):
    if value.size * value.dtype.itemsize <= SMALL:
        return pltpu.with_memory_space_constraint(value, pltpu.VMEM)
    return value


def kernel(body, mib, **kwargs):
    return pl.pallas_call(body, compiler_params=pltpu.CompilerParams(vmem_limit_bytes=mib << 20), **kwargs)


def split_parts(value):
    out = []
    for _ in range(PARTS):
        part = value.astype(BF)
        out.append(part)
        value = value - part.astype(F32)
    return out


def prep_body(q_hbm, g_hbm, o_hbm, n_hbm, out_hbm, q_ref, g_ref, o_ref, n_ref, m_ref, in_sems, out_sems, *, root):
    tokens, heads, _ = q_ref.shape
    seqs = out_hbm.shape[0]
    kvs, rows, _ = m_ref.shape
    group = heads // kvs
    block = tokens * group
    stride = LANES // tokens
    loads = [
        pltpu.make_async_copy(src, dst, in_sems.at[i])
        for i, (src, dst) in enumerate(((n_hbm, n_ref), (g_hbm, g_ref), (o_hbm, o_ref), (q_hbm, q_ref)))
    ]
    for load in loads:
        load.start()
    lane = lax.broadcasted_iota(jnp.int32, (heads, LANES), 1)
    extra = jnp.zeros((heads, LANES), F32)
    pick = lax.broadcasted_iota(jnp.int32, (heads, heads), 0) == lax.broadcasted_iota(
        jnp.int32, (heads, heads), 1
    )
    for load in loads:
        load.wait()
    for t in range(tokens):
        g = g_ref[t].astype(F32)
        o = o_ref[t].astype(F32)
        delta = jnp.sum(g * o, axis=-1, keepdims=True)
        norm_row = jnp.broadcast_to(n_ref[t : t + 1, :], (heads, heads))
        norm = jnp.sum(jnp.where(pick, norm_row, 0.0), axis=-1, keepdims=True) * root
        for p, part in enumerate(split_parts(norm) + split_parts(delta)):
            extra = jnp.where(lane == t * stride + p, part.astype(F32), extra)
    extra = extra.astype(BF)
    for k in range(kvs):
        part = slice(k * group, (k + 1) * group)
        for t in range(tokens):
            m_ref[k, t * group : (t + 1) * group, :] = q_ref[t, part, :]
            m_ref[k, block + t * group : block + (t + 1) * group, :] = g_ref[t, part, :]
        m_ref[k, 2 * block : rows, :] = extra[part, :]
    stores = [pltpu.make_async_copy(m_ref, out_hbm.at[s], out_sems.at[s]) for s in range(seqs)]
    for store in stores:
        store.start()
    for store in stores:
        store.wait()


def unpack(m_ref, first, count, tokens, group):
    block = tokens * group
    stride = LANES // tokens
    q = m_ref[pl.ds(first, count), 0:block, :].reshape(count * block, LANES)
    g = m_ref[pl.ds(first, count), block : 2 * block, :].reshape(count * block, LANES)
    e = m_ref[pl.ds(first, count), 2 * block : 2 * block + group, :]
    lane = lax.broadcasted_iota(jnp.int32, (count, group, LANES), 2)
    pieces = [jnp.where((lane >= t * stride) & (lane < (t + 1) * stride), e, jnp.zeros_like(e)) for t in range(tokens)]
    extra = jnp.stack(pieces, axis=1).reshape(count * block, LANES)
    return q, g, extra


def stage_body(k_ref, v_ref, starts_ref, k_out, v_out, lo_ref, hi_ref, *, tokens, chips, cores, kvs):
    keys = k_ref.shape[0]
    stride = LANES // tokens
    lane = lax.broadcasted_iota(jnp.int32, (keys, LANES), 1) % stride
    minus = jnp.full((keys, LANES), -1.0, F32)
    k_out[:, 0:LANES] = k_ref[...]
    k_out[:, LANES:] = jnp.where(lane < PARTS, minus, 0.0).astype(BF)
    v_out[:, 0:LANES] = v_ref[...]
    v_out[:, LANES:] = jnp.where((lane >= PARTS) & (lane < 2 * PARTS), minus, 0.0).astype(BF)
    core = lax.axis_index("core")
    base = (lax.axis_index("chip") * cores + core) * keys
    each = kvs * tokens
    offset = chips * cores * (keys - each) - base

    def bounds(chip):
        for c in range(cores):
            first = (chip * cores + lax.rem(core + c, cores)) * each
            for t in range(each):
                row = pl.ds(chip * each + t, 1)
                lo_ref[c, row, :] = jnp.full((1, LANES), starts_ref[first + t] - base, jnp.int32)
                hi_ref[c, row, :] = jnp.full((1, LANES), offset + first + t, jnp.int32)

    if chips <= 4:
        for chip in range(chips):
            bounds(chip)
    else:
        pl.loop(0, chips)(bounds)


def grads_body(m_ref, k_ref, v_ref, lo_ref, hi_ref, *rest, tokens, group, step, scaling, turn, last):
    if last:
        done, (w_ref, s_ref, dq_hbm, dq_ref, sems) = rest[:-5], rest[-5:]
    else:
        done, (w_ref, s_ref, dq_ref) = rest[:-3], rest[-3:]
    messages = m_ref.shape[0]
    keys = k_ref.shape[0]
    block = tokens * group
    factor = scaling * math.log2(math.e)
    nt = (((1,), (1,)), ((), ()))
    rows = step * block
    here = step * tokens
    if last:
        cores = dq_hbm.shape[1]
        core = lax.axis_index("core")

        def store(c, src):
            return pltpu.make_async_copy(src, dq_hbm.at[:, lax.rem(core + c, cores)], sems.at[c])

        for c, ref in enumerate(done):
            store(c, ref).start()

    def wide_bounds(ref, at):
        each = [jnp.broadcast_to(ref[turn, pl.ds(at * here + t, 1), :], (group, LANES)) for t in range(here)]
        return jnp.tile(jnp.concatenate(each, axis=0), (1, keys // LANES))

    def visit(at):
        first = pl.ds(at * rows, rows)
        q, g, extra = unpack(m_ref, at * step, step, tokens, group)
        scores = lax.dot_general(jnp.concatenate([q, extra], axis=1), k_ref[...], nt, preferred_element_type=F32)
        pos = lax.broadcasted_iota(jnp.int32, (rows, keys), 1)
        lo, hi = wide_bounds(lo_ref, at), wide_bounds(hi_ref, at)
        weights = jnp.where((pos >= lo) & (pos <= hi), jnp.exp2(scores * factor), 0.0)
        pulled = lax.dot_general(jnp.concatenate([g, extra], axis=1), v_ref[...], nt, preferred_element_type=F32)
        s_half = (weights * pulled).astype(BF)
        w_ref[first, :] = weights.astype(BF)
        s_ref[first, :] = s_half
        dq = jnp.dot(s_half, k_ref[:, 0:LANES], preferred_element_type=F32) * scaling
        dq = dq.astype(BF).reshape(step, block, LANES)
        kvs = dq_ref.shape[1]
        for i in range(step):
            dq_ref[(at * step + i) // kvs, (at * step + i) % kvs] = dq[i]

    steps = messages // step
    if steps <= 4:
        for at in range(steps):
            visit(at)
    else:
        pl.loop(0, steps)(visit)
    if last:
        store(turn, dq_ref).start()
        for c in range(turn):
            store(c, done[c]).wait()
        store(turn, dq_ref).wait()


def context_body(*refs, tokens, group, step, scaling):
    dk_ref, dv_ref = refs[-2:]
    block = tokens * group
    tn = (((0,), (0,)), ((), ()))
    keys = dk_ref.shape[0]
    rows = step * block
    sums = (jnp.zeros((keys, LANES), F32),) * 2
    for m_ref, w_ref, s_ref in zip(refs[0:-2:3], refs[1:-2:3], refs[2:-2:3], strict=True):

        def visit(at, sums):
            first = pl.ds(at * rows, rows)
            q = m_ref[pl.ds(at * step, step), 0:block, :].reshape(rows, LANES)
            g = m_ref[pl.ds(at * step, step), block : 2 * block, :].reshape(rows, LANES)
            dk = lax.dot_general(s_ref[first, :], q, tn, preferred_element_type=F32)
            dv = lax.dot_general(w_ref[first, :], g, tn, preferred_element_type=F32)
            return (sums[0] + dk, sums[1] + dv)

        steps = m_ref.shape[0] // step
        sums = visit(0, sums) if steps == 1 else lax.fori_loop(0, steps, visit, sums)
    dk_ref[...] = (sums[0] * scaling).astype(BF)
    dv_ref[...] = sums[1].astype(BF)


def combine_body(b_ref, dq_ref):
    seqs, kvs, tokens, group, _ = b_ref.shape
    for k in range(kvs):
        for t in range(tokens):
            total = b_ref[0, k, t].astype(F32)
            for s in range(1, seqs):
                total = total + b_ref[s, k, t].astype(F32)
            dq_ref[t, k * group : (k + 1) * group, :] = total.astype(BF)


def local(queries, attn_out, grad_out, log_norms, query_starts, keys, values):
    scaling = queries.shape[-1] ** (-0.5)
    chips, cores, kvs = lax.axis_size("chip"), lax.axis_size("core"), lax.axis_size("kvh")
    senders = chips * kvs
    peers = senders * cores
    tokens, heads, width = queries.shape
    group = heads // kvs
    block = tokens * group
    rows = senders * block
    slow = lambda value: pltpu.with_memory_space_constraint(value, pltpu.HBM)
    rows_sent = 2 * block + group
    message = kernel(
        functools.partial(prep_body, root=1.0 / scaling),
        8,
        out_shape=pltpu.HBM((chips, kvs, rows_sent, width), BF),
        in_specs=[ANY] * 4,
        out_specs=ANY,
        scratch_shapes=[
            pltpu.VMEM(queries.shape, BF),
            pltpu.VMEM(queries.shape, BF),
            pltpu.VMEM(queries.shape, BF),
            pltpu.VMEM(log_norms.shape, F32),
            pltpu.VMEM((kvs, rows_sent, width), BF),
            pltpu.SemaphoreType.DMA((4,)),
            pltpu.SemaphoreType.DMA((chips,)),
        ],
        name="prep",
    )(slow(queries), slow(grad_out), slow(attn_out), slow(log_norms))
    message = message.reshape(senders, rows_sent, width)
    own = lax.all_to_all(message, ("chip", "kvh"), split_axis=0, concat_axis=0, tiled=True)
    key_count = keys.shape[0]
    here = senders * tokens
    k_wide, v_wide, lo, hi = kernel(
        functools.partial(stage_body, tokens=tokens, chips=chips, cores=cores, kvs=kvs),
        8,
        out_shape=(
            held((key_count, 2 * LANES)),
            held((key_count, 2 * LANES)),
            held((cores, here, LANES), jnp.int32),
            held((cores, here, LANES), jnp.int32),
        ),
        in_specs=[VM, VM, pl.BlockSpec(memory_space=pltpu.SMEM)],
        out_specs=(VM,) * 4,
        name="stage",
    )(keys[:, 0, :], values[:, 0, :], slow(query_starts))
    own, k_wide, v_wide, lo, hi = lax.optimization_barrier((own, k_wide, v_wide, lo, hi))
    got = [own]
    for c in range(1, cores):
        got.append(lax.ppermute(own, "core", [((i + c) % cores, i) for i in range(cores)]))
    step = math.gcd(senders, 8)
    partials, context = [], []
    for turn in range(cores):
        last = turn == cores - 1
        scratch = [pltpu.VMEM((chips, kvs, block, width), BF), pltpu.SemaphoreType.DMA((cores,))]
        w, s, partial = kernel(
            functools.partial(
                grads_body, tokens=tokens, group=group, step=step, scaling=scaling, turn=turn, last=last
            ),
            48,
            out_shape=(
                held((rows, key_count)),
                held((rows, key_count)),
                pltpu.HBM((chips, cores, kvs, block, width), BF) if last else held((chips, kvs, block, width)),
            ),
            in_specs=[VM] * (5 + turn),
            out_specs=(VM, VM, ANY if last else VM),
            scratch_shapes=scratch if last else [],
            name=f"grads{turn}",
        )(fast(got[turn]), fast(k_wide), fast(v_wide), fast(lo), fast(hi), *map(fast, partials))
        partials.append(partial)
        context += [fast(got[turn]), fast(w), fast(s)]
    partial = partials[-1].reshape(peers, block, width)
    back = lax.all_to_all(partial, ("chip", "core", "kvh"), split_axis=0, concat_axis=0, tiled=True)
    grad_keys, grad_values = kernel(
        functools.partial(context_body, tokens=tokens, group=group, step=math.gcd(senders, 16), scaling=scaling),
        48,
        out_shape=(jax.ShapeDtypeStruct((key_count, width), BF),) * 2,
        in_specs=[VM] * len(context),
        out_specs=(VM, VM),
        name="context",
    )(*context)
    grad_query = kernel(
        combine_body,
        8,
        out_shape=jax.ShapeDtypeStruct((tokens, heads, width), BF),
        in_specs=[VM],
        out_specs=VM,
        name="combine",
    )(fast(back.reshape(chips * cores, kvs, tokens, group, width)))
    return (grad_query, grad_keys[:, None, :], grad_values[:, None, :])


def solution(mesh):
    seqs, kvs = mesh.shape["seq"], mesh.shape["kvh"]
    cores = 2 if seqs % 2 == 0 else 1
    split = jax.sharding.Mesh(mesh.devices.reshape(seqs // cores, cores, kvs), ("chip", "core", "kvh"))
    token, context = ("chip", "core", "kvh"), ("chip", "core")
    return jax.shard_map(
        local,
        mesh=split,
        in_specs=(
            P(token, None, None),
            P(token, None, None),
            P(token, None, None),
            P(token, None),
            P(),
            P(context, "kvh", None),
            P(context, "kvh", None),
        ),
        out_specs=(P(token, None, None), P(context, "kvh", None), P(context, "kvh", None)),
        check_vma=False,
    )
```

time: 39.6 us -> 34.4 us (0.87)
  local copies, waits for them, and re-layouts: 3.27 us -> 0.01 us
  Pallas kernels: 9.45 us -> 7.71 us
  waiting for transfers between devices: 15.3 us -> 14.6 us
  starting transfers between devices: 10.5 us -> 10.9 us
    broadcast_in_dim x6 -> x0, local copies, waits for them, and re-layouts: 2 us -> none  [the longest x4 1.86 us: local(): jnp.broadcast_to(jnp.repeat(x, group)[:, None], (rows, LANES))]
    pallas_call x3 -> x6, Pallas kernels: 9.45 us -> 7.71 us  [the longest x2 3.02 us: local(): kernel(functools.partial(grads_body, tokens=tokens, group=group, step=ste...]
    all_to_all x2, waiting for transfers between devices: 15.3 us -> 14.4 us  [the longest x1 7.54 us: local(): lax.all_to_all(message, ('chip', 'kvh'), split_axis=0, concat_axis=0, til...]
    unnamed x4, local copies, waits for them, and re-layouts: 0.65 us -> 0.01 us
    convert_element_type x1 -> x0, local copies, waits for them, and re-layouts: 0.61 us -> none  [local(): jnp.sum(back, axis=0).transpose(1, 0, 2, 3).reshape(tokens, heads, width)]
    all_to_all x2, starting transfers between devices: 10.5 us -> 10.9 us  [the longest x1 8.35 us: local(): lax.all_to_all(message, ('chip', 'kvh'), split_axis=0, concat_axis=0, til...]
  transfers between devices with their start and end apart: 2 -> 3, of which waited for: 2 -> 3; matrix products, arithmetic and copies ran while one was open for 1% -> 0% of each run, Pallas kernels for 8% -> 11%
where the time goes in v2:
time: 34.4 us; the launch traced here: 34 us
  waiting for transfers between devices  14.6 us (42%)
  starting transfers between devices  10.9 us (32%)
  Pallas kernels  7.71 us (22%)
  between operations  0.71 us (2%)
    all_to_all x1, starting transfers between devices, local(): lax.all_to_all(message, ('chip', 'kvh'), split_axis=0, concat_axis=0, til...  8.35 us
    all_to_all x1, waiting for transfers between devices, local(): lax.all_to_all(message, ('chip', 'kvh'), split_axis=0, concat_axis=0, til...  7.54 us
    all_to_all x1, waiting for transfers between devices, local(): lax.all_to_all(partial, ('chip', 'core', 'kvh'), split_axis=0, concat_axi...  6.85 us
    pallas_call x2, Pallas kernels, local(): kernel(functools.partial(grads_body, tokens=tokens, group=group, step=ste...  3.02 us
    all_to_all x1, starting transfers between devices, local(): lax.all_to_all(partial, ('chip', 'core', 'kvh'), split_axis=0, concat_axi...  2.58 us
    pallas_call x1, Pallas kernels, local(): kernel(functools.partial(prep_body, root=1.0 / scaling), 8, out_shape=plt...  1.65 us
    pallas_call x1, Pallas kernels, local(): kernel(functools.partial(context_body, tokens=tokens, group=group, step=m...  1.53 us
    pallas_call x1, Pallas kernels, local(): kernel(functools.partial(stage_body, tokens=tokens, chips=chips, cores=co...  0.88 us
  transfers between devices with their start and end apart: 3, of which 3 were waited for; matrix products, arithmetic and copies ran while one was open for 0% of the time, Pallas kernels for 11%

profile of v2, /device:TPU:0, one launch (start us, length us, event | category | flops | bytes accessed | tf_op | source)
XLA Modules:
  0.0 34.0 jit_solution(6992298975881828135)
XLA Ops:
  0.6 0.0 copy-start.1
  0.6 0.0 copy-start
  0.7 1.6 %prep.1 = bf16[4,4,40,128]{3,2,1,0:T(8,128)(2,1)} custom-call(bf16[2,32,128]{2,1,0:T(8,128)(2,1)} %q_hbm.1, bf16[2,32,128]{2,1,0:T(8,128)(2,1)} %g_hbm.1, bf16[2,32,128]{2,1,0:T(8,128)(2,1)} %o_hbm.1, f32[2,32]{1,0:T(2,128)} %n_hbm.1), custom_call_target="tpu_custom_call" | custom-call | tf_op jit(solution)/shard_map/prep/pallas_call | solution.py:230
  2.3 8.4 %all-to-all-start = ((bf16[16,40,128]{2,1,0:T(8,128)(2,1)}), bf16[16,40,128]{2,1,0:T(8,128)(2,1)S(1)}, u32[]{:S(2)}, u32[]{:S(2)}) async-start(bf16[16,40,128]{2,1,0:T(8,128)(2,1)} %bitcast.10), calls=%async_computation | async-start | bytes 327680 | tf_op jit(solution)/shard_map/all_to_all | solution.py:248
  10.7 0.0 copy-done.1
  10.7 0.0 copy-done
  10.7 0.9 %stage.1 = (bf16[1024,256]{1,0:T(8,128)(2,1)S(1)}, bf16[1024,256]{1,0:T(8,128)(2,1)S(1)}, s32[2,32,128]{2,1,0:T(8,128)S(1)}, s32[2,32,128]{2,1,0:T(8,128)S(1)}) custom-call(bf16[1024,128]{1,0:T(8,128)(2,1)S(1)} %bitcast.8, bf16[1024,128]{1,0:T(8,128)(2,1)S(1)} %bitcast.9, s32[64]{0:T(128)} %starts_ref.1), custom_call_target="tpu_custom_call" | custom-call | tf_op jit(solution)/shard_map/stage/pallas_call | solution.py:251
  11.6 7.5 %all-to-all-done.m_ref.refs_0_ = bf16[16,40,128]{2,1,0:T(8,128)(2,1)S(1)} async-done(((bf16[16,40,128]{2,1,0:T(8,128)(2,1)}), bf16[16,40,128]{2,1,0:T(8,128)(2,1)S(1)}, u32[]{:S(2)}, u32[]{:S(2)}) %all-to-all-start) | async-done | bytes 163872 | tf_op jit(solution)/shard_map/all_to_all | solution.py:248
  19.1 0.0 collective-permute-start
  19.1 1.2 %grads0.1 = (bf16[256,1024]{1,0:T(8,128)(2,1)S(1)}, bf16[256,1024]{1,0:T(8,128)(2,1)S(1)}, bf16[4,4,16,128]{3,2,1,0:T(8,128)(2,1)S(1)}) custom-call(bf16[16,40,128]{2,1,0:T(8,128)(2,1)S(1)} %all-to-all-done.m_ref.refs_0_, bf16[1024,256]{1,0:T(8,128)(2,1)S(1)} %get-tuple-element.25.k_ref, bf16[1024,256]{1,0:T(8,128)(2,1)S(1)} %get-tuple-element.26.v_ref, ...), custom_call_target="tpu_custom_call" | custom-call | tf_op jit(solution)/shard_map/grads0/pallas_call | solution.py:273
  20.3 0.2 collective-permute-done.m_ref.refs_3_
  20.5 1.8 %grads1.1 = (bf16[256,1024]{1,0:T(8,128)(2,1)S(1)}, bf16[256,1024]{1,0:T(8,128)(2,1)S(1)}, bf16[4,2,4,16,128]{4,3,2,1,0:T(8,128)(2,1)}) custom-call(bf16[16,40,128]{2,1,0:T(8,128)(2,1)S(1)} %collective-permute-done.m_ref.refs_3_, bf16[1024,256]{1,0:T(8,128)(2,1)S(1)} %get-tuple-element.25.k_ref, bf16[1024,256]{1,0:T(8,128)(2,1)S(1)} %get-tuple-element.26.v_ref, ...), custom_call_target="tpu_custom_call" | custom-call | tf_op jit(solution)/shard_map/grads1/pallas_call | solution.py:273
  22.4 2.6 %all-to-all-start.1 = ((bf16[32,16,128]{2,1,0:T(8,128)(2,1)}), bf16[32,16,128]{2,1,0:T(8,128)(2,1)S(1)}, u32[]{:S(2)}, u32[]{:S(2)}) async-start(bf16[32,16,128]{2,1,0:T(8,128)(2,1)} %bitcast.11), calls=%async_computation.1 | async-start | bytes 262144 | tf_op jit(solution)/shard_map/all_to_all | solution.py:291
  25.0 1.5 %context.1 = (bf16[1024,128]{1,0:T(8,128)(2,1)}, bf16[1024,128]{1,0:T(8,128)(2,1)}) custom-call(bf16[16,40,128]{2,1,0:T(8,128)(2,1)S(1)} %all-to-all-done.m_ref.refs_0_, bf16[256,1024]{1,0:T(8,128)(2,1)S(1)} %get-tuple-element.31.refs_1_, bf16[256,1024]{1,0:T(8,128)(2,1)S(1)} %get-tuple-element.32.refs_2_, ...), custom_call_target="tpu_custom_call" | custom-call | tf_op jit(solution)/shard_map/context/pallas_call | solution.py:292
  26.5 6.8 %all-to-all-done.1 = bf16[32,16,128]{2,1,0:T(8,128)(2,1)S(1)} async-done(((bf16[32,16,128]{2,1,0:T(8,128)(2,1)}), bf16[32,16,128]{2,1,0:T(8,128)(2,1)S(1)}, u32[]{:S(2)}, u32[]{:S(2)}) %all-to-all-start.1) | async-done | bytes 131104 | tf_op jit(solution)/shard_map/all_to_all | solution.py:291
  33.3 0.6 %combine.1 = bf16[2,32,128]{2,1,0:T(8,128)(2,1)} custom-call(bf16[8,4,2,8,128]{4,3,2,1,0:T(8,128)(2,1)S(1)} %bitcast.7), custom_call_target="tpu_custom_call" | custom-call | tf_op jit(solution)/shard_map/combine/pallas_call | solution.py:300
Async XLA Ops:
  0.6 10.0 %copy-start.1 = (bf16[1024,1,128]{2,0,1:T(8,128)(2,1)S(1)}, bf16[1024,1,128]{2,0,1:T(8,128)(2,1)}, u32[]{:S(2)}) copy-start(bf16[1024,1,128]{2,0,1:T(8,128)(2,1)} %param.13) | copy-start | bytes 786436
  0.6 10.0 %copy-start = (bf16[1024,1,128]{2,0,1:T(8,128)(2,1)S(1)}, bf16[1024,1,128]{2,0,1:T(8,128)(2,1)}, u32[]{:S(2)}) copy-start(bf16[1024,1,128]{2,0,1:T(8,128)(2,1)} %param.12) | copy-start | bytes 786436
  2.3 16.8 %all-to-all-start = ((bf16[16,40,128]{2,1,0:T(8,128)(2,1)}), bf16[16,40,128]{2,1,0:T(8,128)(2,1)S(1)}, u32[]{:S(2)}, u32[]{:S(2)}) async-start(bf16[16,40,128]{2,1,0:T(8,128)(2,1)} %bitcast.10), calls=%async_computation | async-start | bytes 327680 | tf_op jit(solution)/shard_map/all_to_all | solution.py:248
  19.1 1.4 %collective-permute-start = (bf16[16,40,128]{2,1,0:T(8,128)(2,1)S(1)}, bf16[16,40,128]{2,1,0:T(8,128)(2,1)S(1)}, u32[]{:S(2)}, u32[]{:S(2)}) collective-permute-start(bf16[16,40,128]{2,1,0:T(8,128)(2,1)S(1)} %all-to-all-done.m_ref.refs_0_), channel_id=1, source_target_pairs={{4,0},{0,4},{5,1},{1,5},{6,2},{2,6},{7,3},{3,7},{12,8},{8,12},{13,... | collective-permute-start | bytes 491528 | tf_op jit(solution)/shard_map/ppermute | solution.py:267
  22.4 11.0 %all-to-all-start.1 = ((bf16[32,16,128]{2,1,0:T(8,128)(2,1)}), bf16[32,16,128]{2,1,0:T(8,128)(2,1)S(1)}, u32[]{:S(2)}, u32[]{:S(2)}) async-start(bf16[32,16,128]{2,1,0:T(8,128)(2,1)} %bitcast.11), calls=%async_computation.1 | async-start | bytes 262144 | tf_op jit(solution)/shard_map/all_to_all | solution.py:291

commit v3 on v2

--- a/solution.py
+++ b/solution.py
@@ -10,6 +10,8 @@
 
 LANES = 128
 PARTS = 3
+STEP = 16
+SPAN = 1024
 BF = jnp.bfloat16
 F32 = jnp.float32
 VM = pl.BlockSpec(memory_space=pltpu.VMEM)
@@ -74,7 +76,8 @@
             extra = jnp.where(lane == t * stride + p, part.astype(F32), extra)
     extra = extra.astype(BF)
     for k in range(kvs):
-        part = slice(k * group, (k + 1) * group)
+        head = kvs - 1 - k
+        part = slice(head * group, (head + 1) * group)
         for t in range(tokens):
             m_ref[k, t * group : (t + 1) * group, :] = q_ref[t, part, :]
             m_ref[k, block + t * group : block + (t + 1) * group, :] = g_ref[t, part, :]
@@ -101,12 +104,12 @@
 def stage_body(k_ref, v_ref, starts_ref, k_out, v_out, lo_ref, hi_ref, *, tokens, chips, cores, kvs):
     keys = k_ref.shape[0]
     stride = LANES // tokens
-    lane = lax.broadcasted_iota(jnp.int32, (keys, LANES), 1) % stride
-    minus = jnp.full((keys, LANES), -1.0, F32)
-    k_out[:, 0:LANES] = k_ref[...]
-    k_out[:, LANES:] = jnp.where(lane < PARTS, minus, 0.0).astype(BF)
-    v_out[:, 0:LANES] = v_ref[...]
-    v_out[:, LANES:] = jnp.where((lane >= PARTS) & (lane < 2 * PARTS), minus, 0.0).astype(BF)
+    row = lax.broadcasted_iota(jnp.int32, (LANES, keys), 0) % stride
+    minus = jnp.full((LANES, keys), -1.0, F32)
+    k_out[0:LANES, :] = k_ref[...].T
+    k_out[LANES:, :] = jnp.where(row < PARTS, minus, 0.0).astype(BF)
+    v_out[0:LANES, :] = v_ref[...].T
+    v_out[LANES:, :] = jnp.where((row >= PARTS) & (row < 2 * PARTS), minus, 0.0).astype(BF)
     core = lax.axis_index("core")
     base = (lax.axis_index("chip") * cores + core) * keys
     each = kvs * tokens
@@ -115,10 +118,11 @@
     def bounds(chip):
         for c in range(cores):
             first = (chip * cores + lax.rem(core + c, cores)) * each
-            for t in range(each):
-                row = pl.ds(chip * each + t, 1)
-                lo_ref[c, row, :] = jnp.full((1, LANES), starts_ref[first + t] - base, jnp.int32)
-                hi_ref[c, row, :] = jnp.full((1, LANES), offset + first + t, jnp.int32)
+            for i in range(each):
+                row = pl.ds(chip * each + i, 1)
+                t = first + (kvs - 1 - i // tokens) * tokens + i % tokens
+                lo_ref[c, row, :] = jnp.full((1, LANES), starts_ref[t] - base, jnp.int32)
+                hi_ref[c, row, :] = jnp.full((1, LANES), offset + t, jnp.int32)
 
     if chips <= 4:
         for chip in range(chips):
@@ -127,17 +131,28 @@
         pl.loop(0, chips)(bounds)
 
 
-def grads_body(m_ref, k_ref, v_ref, lo_ref, hi_ref, *rest, tokens, group, step, scaling, turn, last):
+def visible_bounds(ref, turn, first, count, group, span):
+    each = [jnp.broadcast_to(ref[turn, pl.ds(first + t, 1), :], (group, LANES)) for t in range(count)]
+    return jnp.tile(jnp.concatenate(each, axis=0), (1, span // LANES))
+
+
+def scored(q_wide, g_wide, k_ref, v_ref, part, lo, hi, factor):
+    scores = jnp.dot(q_wide, k_ref[:, part], preferred_element_type=F32)
+    pulled = jnp.dot(g_wide, v_ref[:, part], preferred_element_type=F32)
+    pos = lax.broadcasted_iota(jnp.int32, scores.shape, 1) + part.start
+    weights = jnp.where((pos >= lo) & (pos <= hi), jnp.exp2(scores * factor), 0.0)
+    return weights, weights * pulled
+
+
+def grads_body(m_ref, key_ref, k_ref, v_ref, lo_ref, hi_ref, *rest, tokens, group, step, span, scaling, turn, last):
     if last:
-        done, (w_ref, s_ref, dq_hbm, dq_ref, sems) = rest[:-5], rest[-5:]
+        done, (dq_hbm, dq_ref, sems) = rest[:-3], rest[-3:]
     else:
-        done, (w_ref, s_ref, dq_ref) = rest[:-3], rest[-3:]
+        done, (dq_ref,) = rest[:-1], rest[-1:]
     messages = m_ref.shape[0]
-    keys = k_ref.shape[0]
+    keys = key_ref.shape[0]
     block = tokens * group
     factor = scaling * math.log2(math.e)
-    nt = (((1,), (1,)), ((), ()))
-    rows = step * block
     here = step * tokens
     if last:
         cores = dq_hbm.shape[1]
@@ -149,23 +164,19 @@
         for c, ref in enumerate(done):
             store(c, ref).start()
 
-    def wide_bounds(ref, at):
-        each = [jnp.broadcast_to(ref[turn, pl.ds(at * here + t, 1), :], (group, LANES)) for t in range(here)]
-        return jnp.tile(jnp.concatenate(each, axis=0), (1, keys // LANES))
-
     def visit(at):
-        first = pl.ds(at * rows, rows)
         q, g, extra = unpack(m_ref, at * step, step, tokens, group)
-        scores = lax.dot_general(jnp.concatenate([q, extra], axis=1), k_ref[...], nt, preferred_element_type=F32)
-        pos = lax.broadcasted_iota(jnp.int32, (rows, keys), 1)
-        lo, hi = wide_bounds(lo_ref, at), wide_bounds(hi_ref, at)
-        weights = jnp.where((pos >= lo) & (pos <= hi), jnp.exp2(scores * factor), 0.0)
-        pulled = lax.dot_general(jnp.concatenate([g, extra], axis=1), v_ref[...], nt, preferred_element_type=F32)
-        s_half = (weights * pulled).astype(BF)
-        w_ref[first, :] = weights.astype(BF)
-        s_ref[first, :] = s_half
-        dq = jnp.dot(s_half, k_ref[:, 0:LANES], preferred_element_type=F32) * scaling
-        dq = dq.astype(BF).reshape(step, block, LANES)
+        q_wide = jnp.concatenate([q, extra], axis=1)
+        g_wide = jnp.concatenate([g, extra], axis=1)
+        lo = visible_bounds(lo_ref, turn, at * here, here, group, span)
+        hi = visible_bounds(hi_ref, turn, at * here, here, group, span)
+        dq = None
+        for j in range(keys // span):
+            part = slice(j * span, (j + 1) * span)
+            _, s = scored(q_wide, g_wide, k_ref, v_ref, part, lo, hi, factor)
+            add = jnp.dot(s.astype(BF), key_ref[part, :], preferred_element_type=F32)
+            dq = add if dq is None else dq + add
+        dq = (dq * scaling).astype(BF).reshape(step, block, LANES)
         kvs = dq_ref.shape[1]
         for i in range(step):
             dq_ref[(at * step + i) // kvs, (at * step + i) % kvs] = dq[i]
@@ -183,27 +194,44 @@
         store(turn, dq_ref).wait()
 
 
-def context_body(*refs, tokens, group, step, scaling):
+def context_body(k_ref, v_ref, lo_ref, hi_ref, *refs, tokens, group, step, scaling):
     dk_ref, dv_ref = refs[-2:]
     block = tokens * group
     tn = (((0,), (0,)), ((), ()))
     keys = dk_ref.shape[0]
-    rows = step * block
-    sums = (jnp.zeros((keys, LANES), F32),) * 2
-    for m_ref, w_ref, s_ref in zip(refs[0:-2:3], refs[1:-2:3], refs[2:-2:3], strict=True):
-
-        def visit(at, sums):
-            first = pl.ds(at * rows, rows)
-            q = m_ref[pl.ds(at * step, step), 0:block, :].reshape(rows, LANES)
-            g = m_ref[pl.ds(at * step, step), block : 2 * block, :].reshape(rows, LANES)
-            dk = lax.dot_general(s_ref[first, :], q, tn, preferred_element_type=F32)
-            dv = lax.dot_general(w_ref[first, :], g, tn, preferred_element_type=F32)
-            return (sums[0] + dk, sums[1] + dv)
+    factor = scaling * math.log2(math.e)
+    here = step * tokens
+    whole = slice(0, keys)
+    sums = None
+    for turn, m_ref in enumerate(refs[:-2]):
+
+        def visit(at):
+            q, g, extra = unpack(m_ref, at * step, step, tokens, group)
+            lo = visible_bounds(lo_ref, turn, at * here, here, group, keys)
+            hi = visible_bounds(hi_ref, turn, at * here, here, group, keys)
+            q_wide = jnp.concatenate([q, extra], axis=1)
+            g_wide = jnp.concatenate([g, extra], axis=1)
+            w, s = scored(q_wide, g_wide, k_ref, v_ref, whole, lo, hi, factor)
+            dk = lax.dot_general(s.astype(BF), q, tn, preferred_element_type=F32)
+            dv = lax.dot_general(w.astype(BF), g, tn, preferred_element_type=F32)
+            return dk, dv
+
+        def add(at, sums):
+            return tuple(old + new for old, new in zip(sums, visit(at), strict=True))
 
         steps = m_ref.shape[0] // step
-        sums = visit(0, sums) if steps == 1 else lax.fori_loop(0, steps, visit, sums)
+        sums = visit(0) if sums is None else add(0, sums)
+        if steps > 1:
+            sums = lax.fori_loop(1, steps, add, sums)
     dk_ref[...] = (sums[0] * scaling).astype(BF)
     dv_ref[...] = sums[1].astype(BF)
+
+
+def exchange(value, axes):
+    outer = math.prod(lax.axis_size(a) for a in axes[:-1])
+    inner = lax.axis_size(axes[-1])
+    order = [o * inner + i for o in range(outer) for i in reversed(range(inner))]
+    return lax.all_to_all(value, axes, split_axis=0, concat_axis=0, axis_index_groups=[order], tiled=True)
 
 
 def combine_body(b_ref, dq_ref):
@@ -213,7 +241,8 @@
             total = b_ref[0, k, t].astype(F32)
             for s in range(1, seqs):
                 total = total + b_ref[s, k, t].astype(F32)
-            dq_ref[t, k * group : (k + 1) * group, :] = total.astype(BF)
+            head = kvs - 1 - k
+            dq_ref[t, head * group : (head + 1) * group, :] = total.astype(BF)
 
 
 def local(queries, attn_out, grad_out, log_norms, query_starts, keys, values):
@@ -224,7 +253,6 @@
     tokens, heads, width = queries.shape
     group = heads // kvs
     block = tokens * group
-    rows = senders * block
     slow = lambda value: pltpu.with_memory_space_constraint(value, pltpu.HBM)
     rows_sent = 2 * block + group
     message = kernel(
@@ -245,58 +273,62 @@
         name="prep",
     )(slow(queries), slow(grad_out), slow(attn_out), slow(log_norms))
     message = message.reshape(senders, rows_sent, width)
-    own = lax.all_to_all(message, ("chip", "kvh"), split_axis=0, concat_axis=0, tiled=True)
+    own = exchange(message, ("chip", "kvh"))
     key_count = keys.shape[0]
+    key_rows = fast(keys[:, 0, :])
     here = senders * tokens
     k_wide, v_wide, lo, hi = kernel(
         functools.partial(stage_body, tokens=tokens, chips=chips, cores=cores, kvs=kvs),
         8,
         out_shape=(
-            held((key_count, 2 * LANES)),
-            held((key_count, 2 * LANES)),
+            held((2 * LANES, key_count)),
+            held((2 * LANES, key_count)),
             held((cores, here, LANES), jnp.int32),
             held((cores, here, LANES), jnp.int32),
         ),
         in_specs=[VM, VM, pl.BlockSpec(memory_space=pltpu.SMEM)],
         out_specs=(VM,) * 4,
         name="stage",
-    )(keys[:, 0, :], values[:, 0, :], slow(query_starts))
+    )(key_rows, values[:, 0, :], slow(query_starts))
     own, k_wide, v_wide, lo, hi = lax.optimization_barrier((own, k_wide, v_wide, lo, hi))
     got = [own]
     for c in range(1, cores):
         got.append(lax.ppermute(own, "core", [((i + c) % cores, i) for i in range(cores)]))
-    step = math.gcd(senders, 8)
-    partials, context = [], []
+    step = math.gcd(senders, STEP)
+    partials = []
+    staged = (fast(k_wide), fast(v_wide), fast(lo), fast(hi))
     for turn in range(cores):
         last = turn == cores - 1
         scratch = [pltpu.VMEM((chips, kvs, block, width), BF), pltpu.SemaphoreType.DMA((cores,))]
-        w, s, partial = kernel(
+        partial = kernel(
             functools.partial(
-                grads_body, tokens=tokens, group=group, step=step, scaling=scaling, turn=turn, last=last
+                grads_body,
+                tokens=tokens,
+                group=group,
+                step=step,
+                span=math.gcd(key_count, SPAN),
+                scaling=scaling,
+                turn=turn,
+                last=last,
             ),
-            48,
-            out_shape=(
-                held((rows, key_count)),
-                held((rows, key_count)),
-                pltpu.HBM((chips, cores, kvs, block, width), BF) if last else held((chips, kvs, block, width)),
-            ),
-            in_specs=[VM] * (5 + turn),
-            out_specs=(VM, VM, ANY if last else VM),
+            40,
+            out_shape=pltpu.HBM((chips, cores, kvs, block, width), BF) if last else held((chips, kvs, block, width)),
+            in_specs=[VM] * (6 + turn),
+            out_specs=ANY if last else VM,
             scratch_shapes=scratch if last else [],
             name=f"grads{turn}",
-        )(fast(got[turn]), fast(k_wide), fast(v_wide), fast(lo), fast(hi), *map(fast, partials))
+        )(fast(got[turn]), fast(key_rows), *staged, *map(fast, partials))
         partials.append(partial)
-        context += [fast(got[turn]), fast(w), fast(s)]
     partial = partials[-1].reshape(peers, block, width)
-    back = lax.all_to_all(partial, ("chip", "core", "kvh"), split_axis=0, concat_axis=0, tiled=True)
+    back = exchange(partial, ("chip", "core", "kvh"))
     grad_keys, grad_values = kernel(
-        functools.partial(context_body, tokens=tokens, group=group, step=math.gcd(senders, 16), scaling=scaling),
-        48,
+        functools.partial(context_body, tokens=tokens, group=group, step=step, scaling=scaling),
+        40,
         out_shape=(jax.ShapeDtypeStruct((key_count, width), BF),) * 2,
-        in_specs=[VM] * len(context),
+        in_specs=[VM] * (4 + cores),
         out_specs=(VM, VM),
         name="context",
-    )(*context)
+    )(*staged, *map(fast, got))
     grad_query = kernel(
         combine_body,
         8,

time: 34.4 us -> 31.4 us (0.913)
  the two profiles are of different devices: /device:TPU:0 before, /device:TPU:1 now
where the time goes in v3:
time: 31.4 us; the launch traced here: 31 us
  starting transfers between devices  13.4 us (43%)
  waiting for transfers between devices  9.41 us (30%)
  Pallas kernels  7.5 us (24%)
  between operations  0.7 us (2%)
    all_to_all x2, starting transfers between devices, exchange(): lax.all_to_all(value, axes, split_axis=0, concat_axis=0, axis_index_group...  11.8 us
    all_to_all x2, waiting for transfers between devices, exchange(): lax.all_to_all(value, axes, split_axis=0, concat_axis=0, axis_index_group...  9.07 us
    pallas_call x1, Pallas kernels, local(): kernel(functools.partial(context_body, tokens=tokens, group=group, step=s...  2.34 us
    pallas_call x2, Pallas kernels, local(): kernel(functools.partial(grads_body, tokens=tokens, group=group, step=ste...  2.02 us
    pallas_call x1, Pallas kernels, local(): kernel(functools.partial(prep_body, root=1.0 / scaling), 8, out_shape=plt...  1.65 us
    ppermute x1, starting transfers between devices, local(): lax.ppermute(own, 'core', [((i + c) % cores, i) for i in range(cores)])  1.64 us
    pallas_call x1, Pallas kernels, local(): kernel(functools.partial(stage_body, tokens=tokens, chips=chips, cores=co...  0.86 us
  transfers between devices with their start and end apart: 3, of which 3 were waited for; matrix products, arithmetic and copies ran while one was open for 0% of the time, Pallas kernels for 13%

profile of v3, /device:TPU:1, one launch (start us, length us, event | category | flops | bytes accessed | tf_op | source)
XLA Modules:
  0.0 31.0 jit_solution(12402213834050476181)
XLA Ops:
  0.6 0.0 copy-start
  0.6 0.0 copy-start.1
  0.7 1.6 %prep.1 = bf16[4,4,40,128]{3,2,1,0:T(8,128)(2,1)} custom-call(bf16[2,32,128]{2,1,0:T(8,128)(2,1)} %q_hbm.1, bf16[2,32,128]{2,1,0:T(8,128)(2,1)} %g_hbm.1, bf16[2,32,128]{2,1,0:T(8,128)(2,1)} %o_hbm.1, f32[2,32]{1,0:T(2,128)} %n_hbm.1), custom_call_target="tpu_custom_call" | custom-call | tf_op jit(solution)/shard_map/prep/pallas_call | solution.py:258
  2.3 7.6 %all-to-all-start = ((bf16[16,40,128]{2,1,0:T(8,128)(2,1)}), bf16[16,40,128]{2,1,0:T(8,128)(2,1)S(1)}, u32[]{:S(2)}, u32[]{:S(2)}) async-start(bf16[16,40,128]{2,1,0:T(8,128)(2,1)} %bitcast.12), calls=%async_computation | async-start | bytes 327680 | tf_op jit(solution)/shard_map/all_to_all | solution.py:234
  9.9 0.0 copy-done
  9.9 0.0 copy-done.1
  9.9 0.9 %stage.1 = (bf16[256,1024]{1,0:T(8,128)(2,1)S(1)}, bf16[256,1024]{1,0:T(8,128)(2,1)S(1)}, s32[2,32,128]{2,1,0:T(8,128)S(1)}, s32[2,32,128]{2,1,0:T(8,128)S(1)}) custom-call(bf16[1024,128]{1,0:T(8,128)(2,1)S(1)} %bitcast.7, bf16[1024,128]{1,0:T(8,128)(2,1)S(1)} %bitcast.11, s32[64]{0:T(128)} %starts_ref.1), custom_call_target="tpu_custom_call" | custom-call | tf_op jit(solution)/shard_map/stage/pallas_call | solution.py:280
  10.8 3.6 %all-to-all-done.m_ref.refs_0_ = bf16[16,40,128]{2,1,0:T(8,128)(2,1)S(1)} async-done(((bf16[16,40,128]{2,1,0:T(8,128)(2,1)}), bf16[16,40,128]{2,1,0:T(8,128)(2,1)S(1)}, u32[]{:S(2)}, u32[]{:S(2)}) %all-to-all-start) | async-done | bytes 163872 | tf_op jit(solution)/shard_map/all_to_all | solution.py:234
  14.4 1.6 %collective-permute-start = (bf16[16,40,128]{2,1,0:T(8,128)(2,1)S(1)}, bf16[16,40,128]{2,1,0:T(8,128)(2,1)S(1)}, u32[]{:S(2)}, u32[]{:S(2)}) collective-permute-start(bf16[16,40,128]{2,1,0:T(8,128)(2,1)S(1)} %all-to-all-done.m_ref.refs_0_), channel_id=1, source_target_pairs={{4,0},{0,4},{5,1},{1,5},{6,2},{2,6},{7,3},{3,7},{12,8},{8,12},{13,... | collective-permute-start | bytes 491528 | tf_op jit(solution)/shard_map/ppermute | solution.py:296
  16.0 0.7 %grads0.1.rest_0_ = bf16[4,4,16,128]{3,2,1,0:T(8,128)(2,1)S(1)} custom-call(bf16[16,40,128]{2,1,0:T(8,128)(2,1)S(1)} %all-to-all-done.m_ref.refs_0_, bf16[1024,128]{1,0:T(8,128)(2,1)S(1)} %bitcast.8, bf16[256,1024]{1,0:T(8,128)(2,1)S(1)} %get-tuple-element.19.k_ref, bf16[256,1024]{1,0:T(8,128)(2,1)S(1)} %get-tuple-element.20.v_ref, ...), custom_call_target="tpu_custom_call" | custom-call | tf_op jit(solution)/shard_map/grads0/pallas_call | solution.py:303
  16.7 0.3 %collective-permute-done.m_ref.refs_1_ = bf16[16,40,128]{2,1,0:T(8,128)(2,1)S(1)} collective-permute-done((bf16[16,40,128]{2,1,0:T(8,128)(2,1)S(1)}, bf16[16,40,128]{2,1,0:T(8,128)(2,1)S(1)}, u32[]{:S(2)}, u32[]{:S(2)}) %collective-permute-start) | collective-permute-done | bytes 163872 | tf_op jit(solution)/shard_map/ppermute | solution.py:296
  17.1 1.3 %grads1.1 = bf16[4,2,4,16,128]{4,3,2,1,0:T(8,128)(2,1)} custom-call(bf16[16,40,128]{2,1,0:T(8,128)(2,1)S(1)} %collective-permute-done.m_ref.refs_1_, bf16[1024,128]{1,0:T(8,128)(2,1)S(1)} %bitcast.9, bf16[256,1024]{1,0:T(8,128)(2,1)S(1)} %get-tuple-element.19.k_ref, bf16[256,1024]{1,0:T(8,128)(2,1)S(1)} %get-tuple-element.20.v_ref, ...), custom_call_target="tpu_custom_call" | custom-call | tf_op jit(solution)/shard_map/grads1/pallas_call | solution.py:303
  18.4 4.2 %all-to-all-start.1 = ((bf16[32,16,128]{2,1,0:T(8,128)(2,1)}), bf16[32,16,128]{2,1,0:T(8,128)(2,1)S(1)}, u32[]{:S(2)}, u32[]{:S(2)}) async-start(bf16[32,16,128]{2,1,0:T(8,128)(2,1)} %bitcast.13), calls=%async_computation.1 | async-start | bytes 262144 | tf_op jit(solution)/shard_map/all_to_all | solution.py:234
  22.6 2.3 %context.1 = (bf16[1024,128]{1,0:T(8,128)(2,1)}, bf16[1024,128]{1,0:T(8,128)(2,1)}) custom-call(bf16[256,1024]{1,0:T(8,128)(2,1)S(1)} %get-tuple-element.19.k_ref, bf16[256,1024]{1,0:T(8,128)(2,1)S(1)} %get-tuple-element.20.v_ref, s32[2,32,128]{2,1,0:T(8,128)S(1)} %get-tuple-element.21.lo_ref, s32[2,32,128]{2,1,0:T(8,128)S(1)} %get-tuple-element.22.hi_ref, ...), custom_call_target="tpu_custom_call" | custom-call | tf_op jit(solution)/shard_map/context/pallas_call | solution.py:324
  24.9 5.5 %all-to-all-done.1 = bf16[32,16,128]{2,1,0:T(8,128)(2,1)S(1)} async-done(((bf16[32,16,128]{2,1,0:T(8,128)(2,1)}), bf16[32,16,128]{2,1,0:T(8,128)(2,1)S(1)}, u32[]{:S(2)}, u32[]{:S(2)}) %all-to-all-start.1) | async-done | bytes 131104 | tf_op jit(solution)/shard_map/all_to_all | solution.py:234
  30.4 0.6 %combine.1 = bf16[2,32,128]{2,1,0:T(8,128)(2,1)} custom-call(bf16[8,4,2,8,128]{4,3,2,1,0:T(8,128)(2,1)S(1)} %bitcast.10), custom_call_target="tpu_custom_call" | custom-call | tf_op jit(solution)/shard_map/combine/pallas_call | solution.py:332
Async XLA Ops:
  0.6 9.3 %copy-start = (bf16[1024,1,128]{2,0,1:T(8,128)(2,1)S(1)}, bf16[1024,1,128]{2,0,1:T(8,128)(2,1)}, u32[]{:S(2)}) copy-start(bf16[1024,1,128]{2,0,1:T(8,128)(2,1)} %param.12) | copy-start | bytes 786436
  0.6 9.3 %copy-start.1 = (bf16[1024,1,128]{2,0,1:T(8,128)(2,1)S(1)}, bf16[1024,1,128]{2,0,1:T(8,128)(2,1)}, u32[]{:S(2)}) copy-start(bf16[1024,1,128]{2,0,1:T(8,128)(2,1)} %param.13) | copy-start | bytes 786436
  2.3 12.1 %all-to-all-start = ((bf16[16,40,128]{2,1,0:T(8,128)(2,1)}), bf16[16,40,128]{2,1,0:T(8,128)(2,1)S(1)}, u32[]{:S(2)}, u32[]{:S(2)}) async-start(bf16[16,40,128]{2,1,0:T(8,128)(2,1)} %bitcast.12), calls=%async_computation | async-start | bytes 327680 | tf_op jit(solution)/shard_map/all_to_all | solution.py:234
  14.4 2.7 %collective-permute-start = (bf16[16,40,128]{2,1,0:T(8,128)(2,1)S(1)}, bf16[16,40,128]{2,1,0:T(8,128)(2,1)S(1)}, u32[]{:S(2)}, u32[]{:S(2)}) collective-permute-start(bf16[16,40,128]{2,1,0:T(8,128)(2,1)S(1)} %all-to-all-done.m_ref.refs_0_), channel_id=1, source_target_pairs={{4,0},{0,4},{5,1},{1,5},{6,2},{2,6},{7,3},{3,7},{12,8},{8,12},{13,... | collective-permute-start | bytes 491528 | tf_op jit(solution)/shard_map/ppermute | solution.py:296
  18.4 12.0 %all-to-all-start.1 = ((bf16[32,16,128]{2,1,0:T(8,128)(2,1)}), bf16[32,16,128]{2,1,0:T(8,128)(2,1)S(1)}, u32[]{:S(2)}, u32[]{:S(2)}) async-start(bf16[32,16,128]{2,1,0:T(8,128)(2,1)} %bitcast.13), calls=%async_computation.1 | async-start | bytes 262144 | tf_op jit(solution)/shard_map/all_to_all | solution.py:234
